TPU v7x, 32 devices: a whole 2x2x4 slice. The times are simulated.
32 devices in a mesh: batch: 4 (over z), row: 4 (over x, core), col: 2 (over y).
Axes of the slice: x: 2, y: 2, z: 4, core: 2. Of those that a mesh axis runs over, the one named last changes fastest.
Arguments:
- features: bfloat16 [4, 64, 256, 320], P('batch', 'row', 'col'), may hold values from -6 to 6
- first_kernel: bfloat16 [3, 3, 320, 320], replicated, may hold values from -0.109375 to 0.109375
- second_kernel: bfloat16 [3, 3, 320, 320], replicated, may hold values from -0.109375 to 0.109375
- first_gain: float32 [320], replicated, may hold values from 0.5 to 1.5
- first_shift: float32 [320], replicated, may hold values from -3 to 3
- second_gain: float32 [320], replicated, may hold values from 0.5 to 1.5
- second_shift: float32 [320], replicated, may hold values from -3 to 3
- upstream: bfloat16 [4, 64, 256, 320], P('batch', 'row', 'col'), may hold values from -6 to 6
Outputs:
- input_grad: bfloat16 [4, 64, 256, 320], P('batch', 'row', 'col')
- first_kernel_grad: float32 [3, 3, 320, 320], replicated
- second_kernel_grad: float32 [3, 3, 320, 320], replicated
- norm_param_grads: float32 [4, 320], replicated
All inputs are finite; a program needn't handle non-finite values.
Results may differ from a plain program's by a relative error of at most 0.002.
The roundings to bfloat16 on the way count: a program that leaves them out, or rounds other values in their place, can miss the bound.
Values may be sent and summed in bfloat16 or wider, within the bound.
No kernel may reach another device: no remote copies, remote signals or barrier semaphores. Data moves between devices by JAX's collectives and lax.ppermute only.
A program may use at most 128 MiB of HBM per device.

v0:
```python
import jax
import jax.numpy as jnp
from jax import lax
from jax.sharding import PartitionSpec as P

GROUPS = 32


EPS = 1e-05


def padded_2(cells, sides, width):
    for axis, dim in sides:
        count = lax.axis_size(axis)
        ends = count - 1
        head = lax.slice_in_dim(cells, 0, width, axis=dim)
        tail = lax.slice_in_dim(cells, cells.shape[dim] - width, cells.shape[dim], axis=dim)
        cells = jnp.concatenate(
            [
                lax.ppermute(tail, axis, [(i, (i + 1) % count) for i in range(ends)]),
                cells,
                lax.ppermute(head, axis, [((i + 1) % count, i) for i in range(ends)]),
            ],
            axis=dim,
        )
    return cells


def conv_valid(padded, kernel):
    return lax.conv_general_dilated(
        padded,
        kernel,
        (1, 1),
        "VALID",
        dimension_numbers=("NHWC", "HWIO", "NHWC"),
        preferred_element_type=jnp.float32,
    )


def flipped(kernel):
    return jnp.transpose(jnp.flip(kernel, (0, 1)), (0, 1, 3, 2))


def kernel_grad(padded, gradient):
    height, breadth, chans = (gradient.shape[1], gradient.shape[2], gradient.shape[3])
    flat_grad = gradient.reshape(-1, chans)
    pieces = []
    for offset in range(9):
        across, along = (offset // 3, offset % 3)
        window = padded[:, across : across + height, along : along + breadth, :].reshape(
            -1, padded.shape[3]
        )
        pieces.append(
            lax.dot_general(
                window, flat_grad, (((0,), (0,)), ((), ())), preferred_element_type=jnp.float32
            )
        )
    return jnp.stack(pieces).reshape(3, 3, padded.shape[3], chans)


def group_count(values):
    return (
        values.shape[1]
        * lax.axis_size("row")
        * values.shape[2]
        * lax.axis_size("col")
        * (values.shape[3] // GROUPS)
    )


def moments(values):
    bsize, chans = (values.shape[0], values.shape[3])
    count = group_count(values)
    grouped = values.reshape(bsize, -1, GROUPS, chans // GROUPS)
    totals, squares = lax.psum(
        (jnp.sum(grouped, axis=(1, 3)), jnp.sum(grouped * grouped, axis=(1, 3))), ("row", "col")
    )
    center = totals / count
    spread = squares / count - center * center
    shifted = grouped - center[:, None, :, None]
    rstd = lax.rsqrt(spread + EPS)[:, None, :, None]
    return ((shifted * rstd).reshape(values.shape), rstd)


def silu_grad(grad_act, pre):
    sigma = jax.nn.sigmoid(pre)
    return grad_act * sigma * (1.0 + pre * (1.0 - sigma))


def norm_back(grad_pre, normal, rstd, gain):
    bsize, chans = (grad_pre.shape[0], grad_pre.shape[3])
    count = group_count(grad_pre)
    local_shift = jnp.sum(grad_pre, axis=(1, 2))
    local_gain = jnp.sum(grad_pre * normal, axis=(1, 2))
    shift_sum, gain_sum = lax.psum((local_shift, local_gain), ("row", "col"))
    mean_one = jnp.sum((shift_sum * gain).reshape(bsize, GROUPS, -1), axis=2) / count
    mean_two = jnp.sum((gain_sum * gain).reshape(bsize, GROUPS, -1), axis=2) / count
    scaled = (grad_pre * gain).reshape(bsize, -1, GROUPS, chans // GROUPS)
    normal_grouped = normal.reshape(scaled.shape)
    grad_in = rstd * (
        scaled - mean_one[:, None, :, None] - normal_grouped * mean_two[:, None, :, None]
    )
    return (
        grad_in.reshape(grad_pre.shape),
        jnp.sum(local_gain, axis=0),
        jnp.sum(local_shift, axis=0),
    )


def per_device(
    features,
    first_kernel,
    second_kernel,
    first_gain,
    first_shift,
    second_gain,
    second_shift,
    upstream,
):
    normal_one, rstd_one = moments(features.astype(jnp.float32))
    pre_one = normal_one * first_gain + first_shift
    act_one = jax.nn.silu(pre_one).astype(jnp.bfloat16)
    pad_one = padded_2(act_one, (("row", 1), ("col", 2)), 1)
    hidden = conv_valid(pad_one, first_kernel).astype(jnp.bfloat16)
    normal_two, rstd_two = moments(hidden.astype(jnp.float32))
    pre_two = normal_two * second_gain + second_shift
    act_two = jax.nn.silu(pre_two).astype(jnp.bfloat16)
    stacked = jnp.stack([act_two, upstream])
    rimmed = padded_2(stacked, (("row", 2), ("col", 3)), 1)
    pad_two, pad_upstream = (rimmed[0], rimmed[1])
    second_local = kernel_grad(pad_two, upstream)
    grad_pre_two = silu_grad(conv_valid(pad_upstream, flipped(second_kernel)), pre_two)
    grad_hidden, gain_two, shift_two = norm_back(grad_pre_two, normal_two, rstd_two, second_gain)
    grad_hidden = grad_hidden.astype(jnp.bfloat16)
    pad_grad = padded_2(grad_hidden, (("row", 1), ("col", 2)), 1)
    first_local = kernel_grad(pad_one, grad_hidden)
    grad_pre_one = silu_grad(conv_valid(pad_grad, flipped(first_kernel)), pre_one)
    grad_input, gain_one, shift_one = norm_back(grad_pre_one, normal_one, rstd_one, first_gain)
    input_grad = (upstream.astype(jnp.float32) + grad_input).astype(jnp.bfloat16)
    param_local = jnp.stack([gain_one, shift_one, gain_two, shift_two])
    first_kernel_grad, second_kernel_grad, norm_param_grads = lax.psum(
        (first_local, second_local, param_local), ("batch", "row", "col")
    )
    return (input_grad, first_kernel_grad, second_kernel_grad, norm_param_grads)


def solution(mesh):
    placed = (
        P("batch", "row", "col", None),
        P(),
        P(),
        P(),
        P(),
        P(),
        P(),
        P("batch", "row", "col", None),
    )
    return jax.shard_map(
        per_device,
        mesh=mesh,
        in_specs=placed,
        out_specs=(P("batch", "row", "col", None), P(), P(), P()),
        check_vma=False,
    )
```

profile of v0, /device:TPU:0, one launch (start us, length us, event | category | flops | bytes accessed | tf_op | source)
XLA Modules:
  0.0 457.2 jit_solution(7556419209906225697)
XLA Ops:
  9.6 15.2 %all-reduce.4 = (f32[1,32]{1,0:T(1,128)S(1)}, f32[1,32]{1,0:T(1,128)S(1)}) all-reduce(f32[1,32]{1,0:T(1,128)S(1)} %bitcast.409, f32[1,32]{1,0:T(1,128)S(1)} %bitcast.408), channel_id=1, replica_groups=mesh['batch'=4,'row'=4,'col'=2] {'row','col'}, use_global_device_ids=true, to_apply=%region_5.6 | all-reduce | flops 64 | bytes 512 | tf_op jit(solution)/shard_map/psum | solution.py:75
  39.5 3.3 collective-permute-start.2
  53.9 5.1 %maximum_bitcast_fusion = bf16[18,1,130,320]{2,3,0,1:T(8,128)(2,1)} fusion(bf16[1,18,1,320]{2,3,1,0:T(8,128)(2,1)} %copy.34, bf16[1,1,128,320]{2,3,1,0:T(8,128)(2,1)} %copy-done.10, bf16[1,16,128,320]{2,3,1,0:T(8,128)(2,1)S(1)} %fusion.37, bf16[1,1,128,320]{2,3,1,0:T(8,128)(2,1)} %copy-done.12, bf16[1,18,1,320]{2,3,1,0:T(8,128)(2,1)} %copy.33), kind=kLoop, calls=%fused_computation.37 | loop fusion | flops 7488000 | bytes 2995200 | tf_op jit(solution)/shard_map/concatenate | solution.py:18
  59.0 4.4 copy.69
  66.3 4.2 reshape.318
  72.6 8.5 %fusion.5 = (f32[320]{0:T(512)S(1)}, f32[320]{0:T(512)S(1)}, bf16[16,8,17,320]{3,1,2,0:T(8,128)(2,1)}) fusion(pred[8,17]{0,1:T(8,128)(4,1)S(1)} %copy-done.26, bf16[3,3,320,320]{3,2,1,0:T(8,128)(2,1)S(1)} %copy-done, bf16[18,1,7,2,320]{4,2,3,0,1:T(8,128)(2,1)S(1)} %slice.146, bf16[18,1,8,17,320]{4,2,3,0,1:T(8,128)(2,1)S(1)} %copy.37), kind=kOutput, calls=%fused_computation.13 | convolution fusion | flops 4021626368 | bytes 4966536 | tf_op jit(solution)/shard_map/conv_general_dilated | solution.py:30
  81.5 15.0 %all-reduce.3 = (f32[1,32]{1,0:T(1,128)S(1)}, f32[1,32]{1,0:T(1,128)S(1)}) all-reduce(f32[1,32]{1,0:T(1,128)S(1)} %bitcast.410, f32[1,32]{1,0:T(1,128)S(1)} %bitcast.407), channel_id=1, replica_groups=mesh['batch'=4,'row'=4,'col'=2] {'row','col'}, use_global_device_ids=true, to_apply=%region_8.9 | all-reduce | flops 64 | bytes 512 | tf_op jit(solution)/shard_map/psum | solution.py:75
  108.5 3.4 collective-permute-done.5
  113.0 3.7 fusion.252
  116.7 3.2 copy.40
  119.9 3.2 copy.41
  124.4 5.7 %collective-permute-start.6 = (bf16[2,1,18,1,320]{4,0,3,2,1:T(2,128)(2,1)}, bf16[2,1,18,1,320]{4,0,3,2,1:T(2,128)(2,1)}, u32[]{:S(2)}, u32[]{:S(2)}) collective-permute-start(bf16[2,1,18,1,320]{4,0,3,2,1:T(2,128)(2,1)} %copy.40), channel_id=1, source_target_pairs={{0,1},{2,3},{4,5},{6,7},{8,9},{10,11},{12,13},{14,15},{16,17},{18,... | collective-permute-start | bytes 69128 | tf_op jit(solution)/shard_map/ppermute | solution.py:20
  130.1 6.1 %pad_maximum_fusion.2 = (bf16[1,18,129,320]{2,3,1,0:T(8,128)(2,1)}, bf16[1,18,129,320]{2,3,1,0:T(8,128)(2,1)}) fusion(bf16[1,18,1,320]{2,3,1,0:T(8,128)(2,1)} %copy.34, bf16[1,1,128,320]{2,3,1,0:T(8,128)(2,1)} %copy-done.10, bf16[1,16,128,320]{2,3,1,0:T(8,128)(2,1)S(1)} %fusion.37, bf16[1,1,128,320]{2,3,1,0:T(8,128)(2,1)} %copy-done.12, ...), kind=kLoop, calls=%fused_computation.41 | loop fusion | flops 11888640 | bytes 4469760 | tf_op jit(solution)/shard_map/concatenate | solution.py:18
  142.2 8.4 %pad_maximum_fusion = bf16[2,1,18,130,320]{3,4,2,1,0:T(8,128)(2,1)S(1)} fusion(bf16[2,1,18,1,320]{3,4,2,1,0:T(8,128)(2,1)} %copy.43, bf16[2,1,1,128,320]{3,4,2,1,0:T(8,128)(2,1)} %copy-done.15, bf16[1,1,16,128,320]{3,4,2,1,0:T(8,128)(2,1)} %bitcast.394, bf16[1,1,16,128,320]{3,4,2,1,0:T(8,128)(2,1)} %bitcast.397, bf16[2,1,1,128,320]{3,4,2,1,0:T(8,128)(2,1)} %copy-done.14, ...), kind=kLoop, calls=%fused_computation | loop fusion | flops 17971200 | bytes 5990400 | tf_op jit(solution)/shard_map/concatenate | solution.py:18
  150.6 3.2 slice_bitcast_fusion
  153.8 4.4 copy.70
  161.1 4.3 reshape.327
  168.4 11.7 %fusion.24 = (f32[320]{0:T(512)S(1)}, f32[320]{0:T(512)S(1)}, f32[16,8,17,320]{3,1,2,0:T(8,128)}) fusion(bf16[16,8,17,320]{3,1,2,0:T(8,128)(2,1)S(1)} %copy-done.5, f32[320]{0:T(512)S(1)} %mul.216, f32[320]{0:T(512)S(1)} %sub.116, pred[8,17]{0,1:T(8,128)(4,1)S(1)} %copy-done.27, f32[320]{0:T(512)S(1)} %copy-done.24, f32[320]{0:T(512)S(1)} %copy-done.17, ...), kind=kOutput, calls=%fused_computation.32 | convolution fusion | flops 4029285888 | bytes 7756936 | tf_op jit(solution)/shard_map/conv_general_dilated | solution.py:30
  180.2 15.1 %all-reduce.2 = (f32[1,320]{1,0:T(1,128)S(1)}, f32[1,320]{1,0:T(1,128)}) all-reduce(f32[1,320]{1,0:T(1,128)S(1)} %reduce_sum.188, f32[1,320]{1,0:T(1,128)S(1)} %reduce_sum.185), channel_id=1, replica_groups=mesh['batch'=4,'row'=4,'col'=2] {'row','col'}, use_global_device_ids=true, to_apply=%region_16.17 | all-reduce | flops 640 | bytes 5120 | tf_op jit(solution)/shard_map/psum | solution.py:95
  202.2 3.4 fusion.22
  261.1 4.1 collective-permute-start.10
  276.9 5.3 %maximum_bitcast_fusion.1 = bf16[18,1,130,320]{2,3,0,1:T(8,128)(2,1)} fusion(bf16[1,18,1,320]{2,3,1,0:T(8,128)(2,1)} %copy.56, bf16[1,1,128,320]{2,3,1,0:T(8,128)(2,1)} %collective-permute-done.9, bf16[1,16,128,320]{2,3,1,0:T(8,128)(2,1)} %bitcast.401, bf16[1,1,128,320]{2,3,1,0:T(8,128)(2,1)} %collective-permute-done.8, bf16[1,18,1,320]{2,3,1,0:T(8,128)(2,1)} %copy.55), kind=kLoop, calls=%fused_computation.39 | loop fusion | flops 7488000 | bytes 2995200 | tf_op jit(solution)/shard_map/concatenate | solution.py:18
  282.2 4.4 copy.71
  289.7 4.2 reshape.340
  296.0 8.8 %fusion.68 = f32[16,8,17,320]{3,1,2,0:T(8,128)S(1)} fusion(bf16[3,3,320,320]{3,2,1,0:T(8,128)(2,1)S(1)} %copy-done, bf16[18,1,7,2,320]{4,2,3,0,1:T(8,128)(2,1)S(1)} %slice.159, bf16[18,1,8,17,320]{4,2,3,0,1:T(8,128)(2,1)S(1)} %copy.59, pred[8,17]{0,1:T(8,128)(4,1)S(1)} %copy-done.28), kind=kOutput, calls=%fused_computation.81 | convolution fusion | flops 4016752640 | bytes 6356616 | tf_op jit(solution)/shard_map/conv_general_dilated | solution.py:30
  307.4 3.7 copy.68
  311.1 5.2 %fusion.250 = (f32[320]{0:T(512)S(1)}, f32[320]{0:T(512)S(1)}, f32[1,16,128,320]{2,3,1,0:T(8,128)}) fusion(f32[320]{0:T(512)S(1)} %mul.206, f32[320]{0:T(512)S(1)} %sub.110, bf16[1,16,128,320]{2,3,1,0:T(8,128)(2,1)} %param.8, f32[320]{0:T(512)S(1)} %copy-done.23, f32[320]{0:T(512)S(1)} %copy-done.16, f32[16,1,128,320]{2,3,0,1:T(8,128)} %copy.68), kind=kLoop, calls=%fused_computation.207 | loop fusion | flops 10485120 | bytes 6561280 | tf_op jit(solution)/shard_map/reduce_sum | solution.py:93
  316.2 14.3 %all-reduce.1 = (f32[1,320]{1,0:T(1,128)S(1)}, f32[1,320]{1,0:T(1,128)S(1)}) all-reduce(f32[1,320]{1,0:T(1,128)S(1)} %reduce_sum.191, f32[1,320]{1,0:T(1,128)S(1)} %reduce_sum.194), channel_id=1, replica_groups=mesh['batch'=4,'row'=4,'col'=2] {'row','col'}, use_global_device_ids=true, to_apply=%region_19.20 | all-reduce | flops 640 | bytes 5120 | tf_op jit(solution)/shard_map/psum | solution.py:95
  337.4 41.4 %psum.87 = f32[4,320]{1,0:T(4,128)} all-reduce(f32[4,320]{1,0:T(4,128)S(1)} %pad_maximum_fusion.9), channel_id=1, replica_groups=mesh['batch'=4,'row'=4,'col'=2] {'batch','row','col'}, use_global_device_ids=true, to_apply=%region_26.27 | all-reduce | flops 1280 | bytes 10240 | tf_op jit(solution)/shard_map/psum | solution.py:141
  378.8 4.5 fusion.44
  383.3 59.9 %all-reduce.7.cloned.1.call-done = (f32[3,3,320,320]{3,2,1,0:T(8,128)}, f32[3,3,320,320]{3,2,1,0:T(8,128)}) async-done(((f32[3,3,320,320]{3,2,1,0:T(8,128)}, f32[3,3,320,320]{3,2,1,0:T(8,128)}), (f32[3,3,320,320]{3,2,1,0:T(8,128)}, f32[3,3,320,320]{3,2,1,0:T(8,128)})) %all-reduce.7.cloned.1.call-update) | async-done | bytes 7372816 | tf_op jit(solution)/shard_map/psum | solution.py:141
  443.2 4.8 %copy.90 = f32[3,3,320,320]{3,2,1,0:T(8,128)} copy(f32[3,3,320,320]{3,2,1,0:T(8,128)} %get-tuple-element.50) | data formatting | bytes 7372800
  (195 shorter events, 150.4 us)
Async XLA Ops:
  7.2 65.4 %copy-start = (bf16[3,3,320,320]{3,2,1,0:T(8,128)(2,1)S(1)}, bf16[3,3,320,320]{3,2,1,0:T(8,128)(2,1)}, u32[]{:S(2)}) copy-start(bf16[3,3,320,320]{3,2,1,0:T(8,128)(2,1)} %param.9) | copy-start | bytes 5529604
  7.2 436.0 %all-reduce.7.cloned.1.call-start = ((), (), s32[]{:S(2)}) async-start(), calls=%async_computation | async-start | bytes 17694720 | tf_op jit(solution)/shard_map/psum | solution.py:141
  27.9 3.3 collective-permute-start
  29.9 3.8 collective-permute-start.1
  31.2 2.5 copy-start.12
  39.5 7.8 %collective-permute-start.2 = (bf16[1,18,1,320]{3,1,2,0:T(8,128)(2,1)}, bf16[1,18,1,320]{3,1,2,0:T(8,128)(2,1)}, u32[]{:S(2)}, u32[]{:S(2)}) collective-permute-start(bf16[1,18,1,320]{3,1,2,0:T(8,128)(2,1)} %copy.31), channel_id=1, source_target_pairs={{0,1},{2,3},{4,5},{6,7},{8,9},{10,11},{12,13},{14,15},{16,17},{18,... | collective-permute-start | bytes 34568 | tf_op jit(solution)/shard_map/ppermute | solution.py:20
  45.6 6.0 %collective-permute-start.3 = (bf16[1,18,1,320]{3,1,2,0:T(8,128)(2,1)}, bf16[1,18,1,320]{3,1,2,0:T(8,128)(2,1)}, u32[]{:S(2)}, u32[]{:S(2)}) collective-permute-start(bf16[1,18,1,320]{3,1,2,0:T(8,128)(2,1)} %copy.32), channel_id=1, source_target_pairs={{1,0},{3,2},{5,4},{7,6},{9,8},{11,10},{13,12},{15,14},{17,16},{19,... | collective-permute-start | bytes 34568 | tf_op jit(solution)/shard_map/ppermute | solution.py:22
  103.8 8.7 %copy-start.1 = (bf16[1,16,128,320]{2,3,1,0:T(8,128)(2,1)S(1)}, bf16[1,16,128,320]{2,3,1,0:T(8,128)(2,1)}, u32[]{:S(2)}) copy-start(bf16[1,16,128,320]{2,3,1,0:T(8,128)(2,1)} %param.15) | copy-start | bytes 3932164
  103.8 8.7 %copy-start.3 = (bf16[16,1,128,320]{2,3,0,1:T(8,128)(2,1)S(1)}, bf16[16,1,128,320]{2,3,0,1:T(8,128)(2,1)}, u32[]{:S(2)}) copy-start(bf16[16,1,128,320]{2,3,0,1:T(8,128)(2,1)} %copy.64) | copy-start | bytes 3932164
  105.0 3.5 collective-permute-start.4
  107.0 4.9 %collective-permute-start.5 = (bf16[2,1,1,128,320]{3,4,2,1,0:T(8,128)(2,1)S(1)}, bf16[2,1,1,128,320]{3,4,2,1,0:T(8,128)(2,1)S(1)}, u32[]{:S(2)}, u32[]{:S(2)}) collective-permute-start(bf16[2,1,1,128,320]{3,4,2,1,0:T(8,128)(2,1)S(1)} %get-tuple-element.32), channel_id=1, source_target_pairs={{2,0},{4,2},{6,4},{3,1},{5,3},{7,5},{10,8},{12,10},{14,12},{11,9},... | collective-permute-start | bytes 491528 | tf_op jit(solution)/shard_map/ppermute | solution.py:22
  108.4 3.4 copy-start.14
  123.1 16.1 %collective-permute-start.7 = (bf16[2,1,18,1,320]{4,0,3,2,1:T(2,128)(2,1)}, bf16[2,1,18,1,320]{4,0,3,2,1:T(2,128)(2,1)}, u32[]{:S(2)}, u32[]{:S(2)}) collective-permute-start(bf16[2,1,18,1,320]{4,0,3,2,1:T(2,128)(2,1)} %copy.41), channel_id=1, source_target_pairs={{1,0},{3,2},{5,4},{7,6},{9,8},{11,10},{13,12},{15,14},{17,16},{19,... | collective-permute-start | bytes 69128 | tf_op jit(solution)/shard_map/ppermute | solution.py:22
  124.4 11.9 %collective-permute-start.6 = (bf16[2,1,18,1,320]{4,0,3,2,1:T(2,128)(2,1)}, bf16[2,1,18,1,320]{4,0,3,2,1:T(2,128)(2,1)}, u32[]{:S(2)}, u32[]{:S(2)}) collective-permute-start(bf16[2,1,18,1,320]{4,0,3,2,1:T(2,128)(2,1)} %copy.40), channel_id=1, source_target_pairs={{0,1},{2,3},{4,5},{6,7},{8,9},{10,11},{12,13},{14,15},{16,17},{18,... | collective-permute-start | bytes 69128 | tf_op jit(solution)/shard_map/ppermute | solution.py:20
  165.5 2.9 copy-start.25
  165.5 2.9 copy-start.27
  180.2 16.4 %copy-start.18 = (f32[1,320]{1,0:T(1,128)}, f32[1,320]{1,0:T(1,128)S(1)}, u32[]{:S(2)}) copy-start(f32[1,320]{1,0:T(1,128)S(1)} %reduce_sum.188) | copy-start | bytes 3844
  180.2 16.4 %copy-start.20 = (f32[1,320]{1,0:T(1,128)}, f32[1,320]{1,0:T(1,128)S(1)}, u32[]{:S(2)}) copy-start(f32[1,320]{1,0:T(1,128)S(1)} %reduce_sum.185) | copy-start | bytes 3844
  217.0 37.4 %collective-permute-start.8 = (bf16[1,1,128,320]{2,3,1,0:T(8,128)(2,1)}, bf16[1,1,128,320]{2,3,1,0:T(8,128)(2,1)}, u32[]{:S(2)}, u32[]{:S(2)}) collective-permute-start(bf16[1,1,128,320]{2,3,1,0:T(8,128)(2,1)} %copy.65), channel_id=1, source_target_pairs={{0,2},{2,4},{4,6},{1,3},{3,5},{5,7},{8,10},{10,12},{12,14},{9,11},... | collective-permute-start | bytes 245768 | tf_op jit(solution)/shard_map/ppermute | solution.py:20
  225.9 4.5 copy-start.4
  226.0 4.5 copy-start.13
  226.0 28.5 %collective-permute-start.9 = (bf16[1,1,128,320]{2,3,1,0:T(8,128)(2,1)}, bf16[1,1,128,320]{2,3,1,0:T(8,128)(2,1)}, u32[]{:S(2)}, u32[]{:S(2)}) collective-permute-start(bf16[1,1,128,320]{2,3,1,0:T(8,128)(2,1)} %copy.67), channel_id=1, source_target_pairs={{2,0},{4,2},{6,4},{3,1},{5,3},{7,5},{10,8},{12,10},{14,12},{11,9},... | collective-permute-start | bytes 245768 | tf_op jit(solution)/shard_map/ppermute | solution.py:22
  238.7 4.0 copy-start.6
  261.1 8.1 %collective-permute-start.10 = (bf16[1,18,1,320]{3,1,2,0:T(8,128)(2,1)}, bf16[1,18,1,320]{3,1,2,0:T(8,128)(2,1)}, u32[]{:S(2)}, u32[]{:S(2)}) collective-permute-start(bf16[1,18,1,320]{3,1,2,0:T(8,128)(2,1)} %copy.53), channel_id=1, source_target_pairs={{0,1},{2,3},{4,5},{6,7},{8,9},{10,11},{12,13},{14,15},{16,17},{18,... | collective-permute-start | bytes 34568 | tf_op jit(solution)/shard_map/ppermute | solution.py:20
  268.0 6.6 %collective-permute-start.11 = (bf16[1,18,1,320]{3,1,2,0:T(8,128)(2,1)}, bf16[1,18,1,320]{3,1,2,0:T(8,128)(2,1)}, u32[]{:S(2)}, u32[]{:S(2)}) collective-permute-start(bf16[1,18,1,320]{3,1,2,0:T(8,128)(2,1)} %copy.54), channel_id=1, source_target_pairs={{1,0},{3,2},{5,4},{7,6},{9,8},{11,10},{13,12},{15,14},{17,16},{19,... | collective-permute-start | bytes 34568 | tf_op jit(solution)/shard_map/ppermute | solution.py:22
  307.4 3.7 copy-start.16
  307.4 3.7 copy-start.23
  311.1 25.7 %copy-start.19 = (f32[1,320]{1,0:T(1,128)S(1)}, f32[1,320]{1,0:T(1,128)}, u32[]{:S(2)}) copy-start(f32[1,320]{1,0:T(1,128)} %copy-done.18) | copy-start | bytes 3844
  316.2 14.9 %copy-start.21 = (f32[1,320]{1,0:T(1,128)}, f32[1,320]{1,0:T(1,128)S(1)}, u32[]{:S(2)}) copy-start(f32[1,320]{1,0:T(1,128)S(1)} %reduce_sum.191) | copy-start | bytes 3844
  316.2 14.9 %copy-start.22 = (f32[1,320]{1,0:T(1,128)}, f32[1,320]{1,0:T(1,128)S(1)}, u32[]{:S(2)}) copy-start(f32[1,320]{1,0:T(1,128)S(1)} %reduce_sum.194) | copy-start | bytes 3844
  443.2 4.8 %slice-start = ((s8[4423680]{0:T(1024)(128)(4,1)}), s8[4194304]{0:T(1024)(128)(4,1)S(1)}, s32[]{:S(2)}) async-start(s8[4423680]{0:T(1024)(128)(4,1)} %bitcast.404), calls=%async_computation.1 | async-start | bytes 8388608
  443.2 4.8 %slice-start.1 = ((s8[4423680]{0:T(1024)(128)(4,1)}), s8[229376]{0:T(1024)(128)(4,1)S(1)}, s32[]{:S(2)}) async-start(s8[4423680]{0:T(1024)(128)(4,1)} %bitcast.404), calls=%async_computation.2 | async-start | bytes 458752
  (12 other events, 20.5 us)
Sparse Core Ops, SparseCore 0:
  254.5 188.6 all-reduce.6
where the time goes:
time: 463 us; the launch traced here: 457 us
  local copies, waits for them, and re-layouts  132 us (29%)
  blocking collectives  101 us (22%)
  waiting for transfers between devices  70.3 us (15%)
  other arithmetic  56.9 us (12%)
  matrix products  53.6 us (12%)
  starting transfers between devices  28.7 us (6%)
  between operations  14.9 us (3%)
    psum x1, waiting for transfers between devices, per_device(): lax.psum((first_local, second_local, param_local), ('batch', 'row', 'col'))  59.9 us
    psum x1, blocking collectives, per_device(): lax.psum((first_local, second_local, param_local), ('batch', 'row', 'col'))  41.4 us
    unnamed x72, local copies, waits for them, and re-layouts  36.3 us
    psum x2, blocking collectives, moments(): lax.psum((jnp.sum(grouped, axis=(1, 3)), jnp.sum(grouped * grouped, axis=...  30.2 us
    psum x2, blocking collectives, norm_back(): shift_sum, gain_sum = lax.psum((local_shift, local_gain), ('row', 'col'))  29.3 us
    conv_general_dilated x3, matrix products, conv_valid(): lax.conv_general_dilated(padded, kernel, (1, 1), 'VALID', dimension_numbe...  29 us
    concatenate x7, other arithmetic, padded_2(): jnp.concatenate([lax.ppermute(tail, axis, [(i, (i + 1) % count) for i in...  27.1 us
    dot_general x18, matrix products, kernel_grad(): lax.dot_general(window, flat_grad, (((0,), (0,)), ((), ())), preferred_el...  24.6 us
  transfers between devices with their start and end apart: 13, of which 5 were waited for; matrix products, arithmetic and copies ran while one was open for 24% of the time, Pallas kernels for 0%

commit v1 on v0

v1 whole, which is shorter than its diff:
```python
import functools

import jax
import jax.numpy as jnp
from jax import lax
from jax.experimental import pallas as pl
from jax.experimental.pallas import tpu as pltpu
from jax.sharding import PartitionSpec as P

GROUPS = 32
EPS = 1e-05
F32 = jnp.float32
BF16 = jnp.bfloat16
CHUNK = 4
VMEM = pl.BlockSpec(memory_space=pltpu.VMEM)
SMEM = pl.BlockSpec(memory_space=pltpu.SMEM)
AXES = ("batch", "row", "col")


def call(body, out_shape, n_in, scratch=(), flags=True):
    return pl.pallas_call(
        body,
        out_shape=out_shape,
        in_specs=([SMEM] if flags else []) + [VMEM] * n_in,
        out_specs=jax.tree.map(lambda _: VMEM, out_shape),
        scratch_shapes=list(scratch),
    )


def shape(dims, dtype):
    return jax.ShapeDtypeStruct(dims, dtype)


def group_total(rows):
    chans = rows.shape[1]
    width = chans // GROUPS
    left = lax.broadcasted_iota(jnp.int32, (chans, chans), 0).astype(F32)
    right = lax.broadcasted_iota(jnp.int32, (chans, chans), 1).astype(F32)
    same = jnp.floor((left + 0.5) / width) == jnp.floor((right + 0.5) / width)
    return jnp.dot(
        rows,
        same.astype(F32),
        precision=lax.Precision.HIGHEST,
        preferred_element_type=F32,
    )


def mean_rstd(stats, count):
    total = group_total(stats)
    mean = total[0:1] / count
    spread = total[1:2] / count - mean * mean
    return mean, lax.rsqrt(spread + EPS)


def silu(pre):
    return pre / (1.0 + jnp.exp(-pre))


def silu_slope(pre):
    sigma = 1.0 / (1.0 + jnp.exp(-pre))
    return sigma * (1.0 + pre * (1.0 - sigma))


def pair_rows(first, second):
    rows = lax.broadcasted_iota(jnp.int32, (8, first.shape[1]), 0)
    return jnp.where(rows == 0, first, jnp.where(rows == 1, second, 0.0))


def fold(block):
    return jnp.sum(block.reshape(block.shape[0] // 8, 8, block.shape[1]), axis=0)


def build_taps(flags, core, top, bottom, left, right, taps, line, sides, act):
    high, wide, chans = core.shape
    has_top, has_bottom = flags[0] > 0, flags[1] > 0
    has_left, has_right = flags[2] > 0, flags[3] > 0
    index = lax.broadcasted_iota(jnp.int32, (sides.shape[1], 1), 0)
    inside = ((index > 0) | has_top) & ((index < high + 1) | has_bottom) & (index < high + 2)
    sides[0] = jnp.where(inside & has_left, act(left[...].astype(F32)), 0.0)
    sides[1] = jnp.where(inside & has_right, act(right[...].astype(F32)), 0.0)

    def put(position, cells):
        line[7:8, :] = sides[0, pl.ds(position, 1), :]
        line[8 : 8 + wide, :] = cells
        line[8 + wide : 9 + wide, :] = sides[1, pl.ds(position, 1), :]
        for tap in range(3):
            taps[position, :, tap * chans : (tap + 1) * chans] = line[
                7 + tap : 7 + tap + wide, :
            ].astype(BF16)

    put(0, jnp.where(has_top, act(top[...].astype(F32)), 0.0))
    put(high + 1, jnp.where(has_bottom, act(bottom[...].astype(F32)), 0.0))

    def step(row, carry):
        put(row + 1, act(core[row].astype(F32)))
        return carry

    lax.fori_loop(0, high, step, 0)


def flip_weights(kernel, turned):
    chans = turned.shape[1]
    for across in range(3):
        for along in range(3):
            tap = 3 * (2 - across) + 2 - along
            turned[across, :, along * chans : (along + 1) * chans] = kernel[
                tap * chans : (tap + 1) * chans, :
            ]


def conv_rows(taps, weight, first, rows, turned):
    wide, depth = taps.shape[1], taps.shape[2]
    total = None
    for across in range(3):
        cells = taps[pl.ds(first + across, rows)].reshape(rows * wide, depth)
        dims = (((1,), (1 if turned else 0,)), ((), ()))
        part = lax.dot_general(cells, weight(across), dims, preferred_element_type=F32)
        total = part if total is None else total + part
    return total


def look_kernel(flags, core, upstream, stats, tops, bottoms, lefts, rights, edge):
    high, wide, chans = core.shape

    def step(row, carry):
        cells = core[row].astype(F32)
        return carry[0] + fold(cells), carry[1] + fold(cells * cells)

    zero = jnp.zeros((8, chans), F32)
    total, square = lax.fori_loop(0, high, step, (zero, zero))
    stats[...] = pair_rows(
        jnp.sum(total, axis=0, keepdims=True), jnp.sum(square, axis=0, keepdims=True)
    )
    for which, array in enumerate((core, upstream)):
        tops[which] = array[0]
        bottoms[which] = array[high - 1]
        for target, at in ((lefts, 0), (rights, wide - 8)):
            inner = 0 if at == 0 else 7
            for row in range(high):
                strip = array[row, at : at + 8, :].astype(F32)
                edge[row : row + 1, :] = strip[inner : inner + 1, :]
            target[which] = edge[...].astype(BF16)


def sides_kernel(edges, above, below, out, line, *, at):
    count, high, chans = edges.shape
    out_high = out.shape[1]
    inner = 0 if at == 0 else 7
    for which in range(count):
        line[...] = jnp.zeros_like(line)
        line[0:1, :] = above[which, at : at + 8, :].astype(F32)[inner : inner + 1, :]
        line[1 : 1 + high, :] = edges[which].astype(F32)
        line[1 + high : 2 + high, :] = below[which, at : at + 8, :].astype(F32)[
            inner : inner + 1, :
        ]
        out[which] = line[...].astype(BF16)


def identity(cells):
    return cells


def hidden_kernel(
    flags, core, top, bottom, left, right, kernel, stats, gain, shift,
    hidden, sums, taps, line, sides, *, count,
):
    high, wide, chans = core.shape
    mean, rstd = mean_rstd(stats[...], count)
    scale = rstd * gain[...]
    offset = shift[...] - mean * scale
    build_taps(
        flags, core, top, bottom, left, right, taps, line, sides,
        lambda cells: silu(cells * scale + offset),
    )
    depth = taps.shape[2]

    def step(index, carry):
        block = conv_rows(
            taps,
            lambda across: kernel[across * depth : (across + 1) * depth, :],
            index * CHUNK, CHUNK, False,
        ).astype(BF16)
        hidden[pl.ds(index * CHUNK * wide, CHUNK * wide), :] = block
        wideb = block.astype(F32)
        return carry[0] + fold(wideb), carry[1] + fold(wideb * wideb)

    zero = jnp.zeros((8, chans), F32)
    total, square = lax.fori_loop(0, high // CHUNK, step, (zero, zero))
    sums[...] = pair_rows(
        jnp.sum(total, axis=0, keepdims=True), jnp.sum(square, axis=0, keepdims=True)
    )


def back_conv_kernel(
    flags, core, top, bottom, left, right, kernel, out, taps, line, sides, turned
):
    high, wide, chans = core.shape
    build_taps(flags, core, top, bottom, left, right, taps, line, sides, identity)
    flip_weights(kernel, turned)

    def step(index, carry):
        out[pl.ds(index * CHUNK * wide, CHUNK * wide), :] = conv_rows(
            taps, lambda across: turned[across], index * CHUNK, CHUNK, True
        )
        return carry

    lax.fori_loop(0, high // CHUNK, step, 0)


def slope_kernel(grad, hidden, stats, gain, shift, out, sums, *, count):
    mean, rstd = mean_rstd(stats[...], count)
    chans = grad.shape[1]
    size = 256

    def step(index, carry):
        window = pl.ds(index * size, size)
        normal = (hidden[window, :].astype(F32) - mean) * rstd
        block = grad[window, :] * silu_slope(normal * gain[...] + shift[...])
        out[window, :] = block
        return carry[0] + fold(block), carry[1] + fold(block * normal)

    zero = jnp.zeros((8, chans), F32)
    total, product = lax.fori_loop(0, grad.shape[0] // size, step, (zero, zero))
    sums[...] = pair_rows(
        jnp.sum(total, axis=0, keepdims=True), jnp.sum(product, axis=0, keepdims=True)
    )


def norm_back_terms(stats, sums, gain, count):
    mean, rstd = mean_rstd(stats[...], count)
    means = group_total(sums[...] * gain[...]) / count
    return mean, rstd, means[0:1], means[1:2]


def grad_hidden_kernel(
    grad_pre, hidden, stats, sums, gain, out, tops, bottoms, lefts, rights, edge, *, count
):
    mean, rstd, mean_one, mean_two = norm_back_terms(stats, sums, gain, count)
    high, wide, chans = out.shape

    def step(row, carry):
        window = pl.ds(row * wide, wide)
        normal = (hidden[window, :].astype(F32) - mean) * rstd
        block = rstd * (grad_pre[window, :] * gain[...] - mean_one - normal * mean_two)
        out[row] = block.astype(BF16)
        return carry

    lax.fori_loop(0, high, step, 0)
    tops[0] = out[0]
    bottoms[0] = out[high - 1]
    for target, at in ((lefts, 0), (rights, wide - 8)):
        inner = 0 if at == 0 else 7
        for row in range(high):
            strip = out[row, at : at + 8, :].astype(F32)
            edge[row : row + 1, :] = strip[inner : inner + 1, :]
        target[0] = edge[...].astype(BF16)


def input_grad_kernel(grad_pre, core, upstream, stats, sums, gain, out, *, count):
    mean, rstd, mean_one, mean_two = norm_back_terms(stats, sums, gain, count)
    high, wide, chans = out.shape

    def step(row, carry):
        window = pl.ds(row * wide, wide)
        normal = (core[row].astype(F32) - mean) * rstd
        block = rstd * (grad_pre[window, :] * gain[...] - mean_one - normal * mean_two)
        out[row] = (upstream[row].astype(F32) + block).astype(BF16)
        return carry

    lax.fori_loop(0, high, step, 0)


def scatter_blocks(places, natural, out, size):
    for block in range(out.shape[0] // size):
        at = pl.multiple_of(places[block] * size, 8)
        out[block * size : (block + 1) * size, :] = natural[pl.ds(at, size), :]


def second_grad_kernel(
    flags, places, core, top, bottom, left, right, hidden, stats, gain, shift,
    out, taps, line, sides, turned, natural, *, count, size,
):
    high, wide, chans = core.shape
    build_taps(flags, core, top, bottom, left, right, taps, line, sides, identity)
    mean, rstd = mean_rstd(stats[...], count)
    scale = rstd * gain[...]
    offset = shift[...] - mean * scale
    depth = taps.shape[2]
    for part in range(high * wide // 256):
        window = slice(part * 256, (part + 1) * 256)
        act = silu(hidden[window, :].astype(F32) * scale + offset)
        turned[:, window] = act.astype(BF16).T
    for across in range(3):
        cells = taps[2 - across : 2 - across + high].reshape(high * wide, depth)
        block = jnp.dot(turned[...], cells, preferred_element_type=F32)
        for along in range(3):
            lanes = slice((2 - along) * chans, (3 - along) * chans)
            first = (3 * across + along) * chans
            natural[first : first + chans, :] = block[:, lanes]
    natural[9 * chans :, :] = jnp.zeros_like(natural[9 * chans :, :])
    scatter_blocks(places, natural, out, size)


def first_grad_kernel(
    flags, places, core, top, bottom, left, right, grad_hidden, stats, gain, shift,
    out, taps, line, sides, turned, natural, *, count, size,
):
    high, wide, chans = core.shape
    mean, rstd = mean_rstd(stats[...], count)
    scale = rstd * gain[...]
    offset = shift[...] - mean * scale
    build_taps(
        flags, core, top, bottom, left, right, taps, line, sides,
        lambda cells: silu(cells * scale + offset),
    )
    depth = taps.shape[2]
    for part in range(high * wide // 256):
        rows = 256 // wide
        cells = grad_hidden[part * rows : (part + 1) * rows].reshape(256, chans)
        turned[:, part * 256 : (part + 1) * 256] = cells.T
    for across in range(3):
        cells = taps[across : across + high].reshape(high * wide, depth)
        block = jnp.dot(turned[...], cells, preferred_element_type=F32)
        natural[across * depth : (across + 1) * depth, :] = block.T
    natural[9 * chans :, :] = jnp.zeros_like(natural[9 * chans :, :])
    scatter_blocks(places, natural, out, size)


def spread_kernel(places, mine, out, natural, *, size):
    for block in range(mine.shape[0] // size):
        at = pl.multiple_of(places[block] * size, 8)
        natural[pl.ds(at, size), :] = mine[block * size : (block + 1) * size, :].astype(F32)
    out[...] = natural[: out.shape[0], :]


def swap(value, axis, mask):
    return lax.ppermute(value, axis, [(i, i ^ mask) for i in range(lax.axis_size(axis))])


def bits_of(axis):
    count = lax.axis_size(axis)
    assert count & (count - 1) == 0
    return [(axis, 1 << bit) for bit in range(count.bit_length() - 1)]


def add_up(value, axes):
    for axis in axes:
        for name, mask in bits_of(axis):
            value = value + swap(value, name, mask)
    return value


def shifted(value, axis, step):
    count = lax.axis_size(axis)
    pairs = [(i, i + step) for i in range(count) if 0 <= i + step < count]
    return lax.ppermute(value, axis, pairs)


def borders(tops, bottoms, lefts, rights):
    count, wide, chans = tops.shape
    high = lefts.shape[1]
    above = shifted(bottoms, "row", 1)
    below = shifted(tops, "row", -1)

    def column(edges, at):
        return call(
            functools.partial(sides_kernel, at=at),
            shape((count, high + 8, chans), BF16), 3,
            [pltpu.VMEM((high + 8, chans), F32)], flags=False,
        )(edges, above, below)

    from_left = shifted(column(rights, wide - 8), "col", 1)
    from_right = shifted(column(lefts, 0), "col", -1)
    return above, below, from_left, from_right


def plan():
    row, col, batch = bits_of("row"), bits_of("col"), bits_of("batch")
    return row[:1], row[1:] + col, batch


def exchange_orders():
    first, middle, last = plan()
    return (first + middle + last, first + middle[::-1] + last)


def places_of(blocks):
    half = blocks // 2
    levels = len(exchange_orders()[0])
    head = len(plan()[0])
    found = []
    for order in exchange_orders():
        own = 0
        for level, (axis, mask) in enumerate(order):
            bit = (lax.axis_index(axis) & mask) // mask
            weight = half >> (level + 1)
            if level < head:
                weight *= 2
            own = own + bit * weight
        found.append(own)
    outer = blocks >> head
    index = jnp.arange(blocks, dtype=jnp.int32)
    chunk = (index % outer) // (outer // 2)
    return index ^ jnp.where(chunk == 0, found[0], found[1])


def give_away(whole):
    first, middle, last = plan()
    for axis, mask in first:
        half = whole.shape[0] // 2
        whole = whole[:half] + swap(whole[half:], axis, mask)
    half = whole.shape[0] // 2
    chunks = [whole[:half], whole[half:]]
    for pair in zip(middle, middle[::-1], strict=True):
        chunks = [
            chunk[: chunk.shape[0] // 2] + swap(chunk[chunk.shape[0] // 2 :], axis, mask)
            for chunk, (axis, mask) in zip(chunks, pair, strict=True)
        ]
    both = jnp.stack(chunks)
    for axis, mask in last:
        half = both.shape[1] // 2
        both = both[:, :half] + swap(both[:, half:], axis, mask)
    return both


def collect(both):
    first, middle, last = plan()
    for axis, mask in last[::-1]:
        both = jnp.concatenate([both, swap(both, axis, mask)], axis=1)
    chunks = [both[0], both[1]]
    for pair in list(zip(middle, middle[::-1], strict=True))[::-1]:
        chunks = [
            jnp.concatenate([chunk, swap(chunk, axis, mask)])
            for chunk, (axis, mask) in zip(chunks, pair, strict=True)
        ]
    whole = jnp.concatenate(chunks)
    for axis, mask in first[::-1]:
        whole = jnp.concatenate([whole, swap(whole, axis, mask)])
    return whole


def per_device(
    features, first_kernel, second_kernel, first_gain, first_shift,
    second_gain, second_shift, upstream,
):
    high, wide, chans = features.shape[1:]
    rows, cols = lax.axis_size("row"), lax.axis_size("col")
    devices = rows * cols * lax.axis_size("batch")
    count = float(high * rows * wide * cols * (chans // GROUPS))
    cells = features[0]
    upper = upstream[0]
    weights = [k.reshape(9 * chans, chans) for k in (first_kernel, second_kernel)]
    gains = [g.reshape(1, chans) for g in (first_gain, second_gain)]
    shifts = [s.reshape(1, chans) for s in (first_shift, second_shift)]
    row, col = lax.axis_index("row"), lax.axis_index("col")
    flags = jnp.stack([row > 0, row < rows - 1, col > 0, col < cols - 1]).astype(jnp.int32)
    unit = 2 * devices * 16
    padded = -(-9 * chans // unit) * unit
    blocks = 2 * devices
    size = padded // blocks
    places = places_of(blocks)

    image = shape((high, wide, chans), BF16)
    flat = high * wide
    small = shape((8, chans), F32)
    rows_of = lambda n: shape((n, wide, chans), BF16)
    cols_of = lambda n: shape((n, high, chans), BF16)
    edge = pltpu.VMEM((high, chans), F32)
    tap_scratch = [
        pltpu.VMEM((high + 2, wide, 3 * chans), BF16),
        pltpu.VMEM((wide + 16, chans), F32),
        pltpu.VMEM((2, high + 8, chans), F32),
    ]

    stats_one, tops, bottoms, lefts, rights = call(
        look_kernel, (small, rows_of(2), rows_of(2), cols_of(2), cols_of(2)), 2, [edge]
    )(flags, cells, upper)
    above, below, from_left, from_right = borders(tops, bottoms, lefts, rights)
    halo_one = (above[0], below[0], from_left[0], from_right[0])
    halo_up = (above[1], below[1], from_left[1], from_right[1])
    stats_one = add_up(stats_one, ("row", "col"))

    hidden, stats_two = call(
        functools.partial(hidden_kernel, count=count),
        (shape((flat, chans), BF16), small), 9, tap_scratch,
    )(flags, cells, *halo_one, weights[0], stats_one, gains[0], shifts[0])
    stats_two = add_up(stats_two, ("row", "col"))

    back_conv = call(
        back_conv_kernel, shape((flat, chans), F32), 6,
        tap_scratch + [pltpu.VMEM((3, chans, 3 * chans), BF16)],
    )
    grad_act_two = back_conv(flags, upper, *halo_up, weights[1])

    slope = call(
        functools.partial(slope_kernel, count=count),
        (shape((flat, chans), F32), small), 5, flags=False,
    )
    grad_pre_two, local_two = slope(grad_act_two, hidden, stats_two, gains[1], shifts[1])
    sums_two = add_up(local_two, ("row", "col"))

    def kernel_grad_call(body):
        return pl.pallas_call(
            functools.partial(body, count=count, size=size),
            out_shape=shape((padded, chans), F32),
            in_specs=[SMEM, SMEM] + [VMEM] * 9,
            out_specs=VMEM,
            scratch_shapes=tap_scratch
            + [pltpu.VMEM((chans, flat), BF16), pltpu.VMEM((padded, chans), F32)],
        )

    second_local = kernel_grad_call(second_grad_kernel)(
        flags, places, upper, *halo_up, hidden, stats_two, gains[1], shifts[1]
    )
    second_part = give_away(second_local)

    grad_hidden, tops, bottoms, lefts, rights = call(
        functools.partial(grad_hidden_kernel, count=count),
        (image, rows_of(1), rows_of(1), cols_of(1), cols_of(1)), 5, [edge], flags=False,
    )(grad_pre_two, hidden, stats_two, sums_two, gains[1])
    halo_grad = [part[0] for part in borders(tops, bottoms, lefts, rights)]

    first_local = kernel_grad_call(first_grad_kernel)(
        flags, places, cells, *halo_one, grad_hidden, stats_one, gains[0], shifts[0]
    )
    first_part = give_away(first_local)

    grad_act_one = back_conv(flags, grad_hidden, *halo_grad, weights[0])
    grad_pre_one, local_one = slope(
        grad_act_one, cells.reshape(flat, chans), stats_one, gains[0], shifts[0]
    )
    sums_one = add_up(local_one, ("row", "col"))
    input_grad = call(
        functools.partial(input_grad_kernel, count=count), image, 6, flags=False
    )(grad_pre_one, cells, upper, stats_one, sums_one, gains[0])

    param = jnp.stack([sums_one[1], sums_one[0], sums_two[1], sums_two[0]])
    param = add_up(param, ("batch",))

    spread = pl.pallas_call(
        functools.partial(spread_kernel, size=size),
        out_shape=shape((9 * chans, chans), F32),
        in_specs=[SMEM, VMEM],
        out_specs=VMEM,
        scratch_shapes=[pltpu.VMEM((padded, chans), F32)],
    )
    grads = [
        spread(places, collect(part.astype(BF16))).reshape(3, 3, chans, chans)
        for part in (first_part, second_part)
    ]
    return (input_grad[None], grads[0], grads[1], param)


def solution(mesh):
    tiled = P("batch", "row", "col", None)
    return jax.shard_map(
        per_device,
        mesh=mesh,
        in_specs=(tiled, P(), P(), P(), P(), P(), P(), tiled),
        out_specs=(tiled, P(), P(), P()),
        check_vma=False,
    )
```

time: 463 us -> 342 us (0.74); the launches traced: 457 us -> 341 us
  Pallas kernels: 0 us -> 110 us
  blocking collectives: 101 us -> 0 us
  local copies, waits for them, and re-layouts: 132 us -> 64.5 us
  matrix products: 53.6 us -> 0 us
  starting transfers between devices: 28.7 us -> 71.4 us
  other arithmetic: 56.9 us -> 20.4 us
  between operations: 14.9 us -> 1.15 us
    pallas_call x0 -> x16, Pallas kernels: none -> 110 us  [the longest x1 14.7 us: per_device(): call(functools.partial(hidden_kernel, count=count), (shape((flat, chans),...]
    psum x5 -> x0, blocking collectives: 101 us -> none  [the longest x1 41.4 us: per_device(): lax.psum((first_local, second_local, param_local), ('batch', 'row', 'col'))]
    ppermute x12 -> x50, waiting for transfers between devices: 10.4 us -> 73.2 us  [the longest x42 64.6 us: swap(): lax.ppermute(value, axis, [(i, i ^ mask) for i in range(lax.axis_size(axi...]
    psum x1 -> x0, waiting for transfers between devices: 59.9 us -> none  [per_device(): lax.psum((first_local, second_local, param_local), ('batch', 'row', 'col'))]
    ppermute x12 -> x50, starting transfers between devices: 28.7 us -> 71.4 us  [the longest x42 54.9 us: swap(): lax.ppermute(value, axis, [(i, i ^ mask) for i in range(lax.axis_size(axi...]
    conv_general_dilated x3 -> x0, matrix products: 29 us -> none  [conv_valid(): lax.conv_general_dilated(padded, kernel, (1, 1), 'VALID', dimension_numbe...]
    concatenate x7 -> x8, other arithmetic: 27.1 us -> 1.7 us  [the longest x4 1.59 us: collect(): jnp.concatenate([chunk, swap(chunk, axis, mask)])]
    dot_general x18 -> x0, matrix products: 24.6 us -> none  [kernel_grad(): lax.dot_general(window, flat_grad, (((0,), (0,)), ((), ())), preferred_el...]
  transfers between devices with their start and end apart: 13 -> 50, of which waited for: 5 -> 25; matrix products, arithmetic and copies ran while one was open for 24% -> 19% of each run, Pallas kernels for 0% -> 22%
where the time goes in v1:
time: 342 us; the launch traced here: 341 us
  Pallas kernels  110 us (32%)
  waiting for transfers between devices  73.2 us (21%)
  starting transfers between devices  71.4 us (21%)
  local copies, waits for them, and re-layouts  64.5 us (19%)
  other arithmetic  20.4 us (6%)
    ppermute x42, waiting for transfers between devices, swap(): lax.ppermute(value, axis, [(i, i ^ mask) for i in range(lax.axis_size(axi...  64.6 us
    ppermute x42, starting transfers between devices, swap(): lax.ppermute(value, axis, [(i, i ^ mask) for i in range(lax.axis_size(axi...  54.9 us
    unnamed x53, local copies, waits for them, and re-layouts  21.2 us
    ppermute x8, starting transfers between devices, shifted(): return lax.ppermute(value, axis, pairs)  16.5 us
    pallas_call x1, Pallas kernels, per_device(): call(functools.partial(hidden_kernel, count=count), (shape((flat, chans),...  14.7 us
    pallas_call x1, Pallas kernels, per_device(): grad_act_one = back_conv(flags, grad_hidden, *halo_grad, weights[0])  13.9 us
    pallas_call x1, Pallas kernels, per_device(): grad_act_two = back_conv(flags, upper, *halo_up, weights[1])  13.6 us
    pallas_call x1, Pallas kernels, per_device(): kernel_grad_call(first_grad_kernel)  13.2 us
  transfers between devices with their start and end apart: 50, of which 25 were waited for; matrix products, arithmetic and copies ran while one was open for 19% of the time, Pallas kernels for 22%

profile of v1, /device:TPU:0, one launch (start us, length us, event | category | flops | bytes accessed | tf_op | source)
XLA Modules:
  0.0 340.9 jit_solution(15190162046253526764)
XLA Ops:
  0.7 2.6 copy.17
  5.5 3.1 shard_map.111
  8.6 2.4 collective-permute-start
  12.3 3.3 collective-permute-start.4
  28.0 3.4 %collective-permute-start.2 = (bf16[2,24,320]{2,1,0:T(8,128)(2,1)}, bf16[2,24,320]{2,1,0:T(8,128)(2,1)S(1)}, u32[]{:S(2)}, u32[]{:S(2)}) collective-permute-start(bf16[2,24,320]{2,1,0:T(8,128)(2,1)} %shard_map.112), channel_id=1, source_target_pairs={{0,1},{2,3},{4,5},{6,7},{8,9},{10,11},{12,13},{14,15},{16,17},{18,... | collective-permute-start | bytes 92168 | tf_op jit(solution)/shard_map/ppermute | solution.py:356
  39.8 14.7 %shard_map.115 = (bf16[2048,320]{1,0:T(8,128)(2,1)}, f32[8,320]{1,0:T(8,128)}) custom-call(s32[4]{0:T(128)} %add_convert_fusion.flags, bf16[16,128,320]{2,1,0:T(8,128)(2,1)} %bitcast.65, bf16[128,320]{1,0:T(8,128)(2,1)} %get-tuple-element.70.top, bf16[128,320]{1,0:T(8,128)(2,1)} %get-tuple-element.68.bottom, bf16[24,320]{1,0:T(8,128)(2,1)} %get-tuple-element.82.left, ...), custom_call_target="tpu_custom_call" | custom-call | tf_op jit(solution)/shard_map/pallas_call | solution.py:483
  64.6 12.2 %shard_map.125 = f32[3072,320]{1,0:T(8,128)} custom-call(s32[4]{0:T(128)} %add_convert_fusion.flags, s32[64]{0:T(128)} %fusion.10.places, bf16[16,128,320]{2,1,0:T(8,128)(2,1)} %bitcast.70, bf16[128,320]{1,0:T(8,128)(2,1)} %get-tuple-element.71.top, bf16[128,320]{1,0:T(8,128)(2,1)} %get-tuple-element.69.bottom, bf16[24,320]{1,0:T(8,128)(2,1)} %get-tuple-element.83.left, ...), custom_call_target="tpu_custom_call" | custom-call | tf_op jit(solution)/shard_map/pallas_call | solution.py:512
  80.3 13.6 %shard_map.114.grad = f32[2048,320]{1,0:T(8,128)} custom-call(s32[4]{0:T(128)} %add_convert_fusion.flags, bf16[16,128,320]{2,1,0:T(8,128)(2,1)} %bitcast.71, bf16[128,320]{1,0:T(8,128)(2,1)} %get-tuple-element.71.top, bf16[128,320]{1,0:T(8,128)(2,1)} %get-tuple-element.69.bottom, bf16[24,320]{1,0:T(8,128)(2,1)} %get-tuple-element.83.left, ...), custom_call_target="tpu_custom_call" | custom-call | tf_op jit(solution)/shard_map/pallas_call | solution.py:493
  93.9 6.5 %shard_map.116 = (f32[2048,320]{1,0:T(8,128)}, f32[8,320]{1,0:T(8,128)}) custom-call(f32[2048,320]{1,0:T(8,128)} %shard_map.114.grad, bf16[2048,320]{1,0:T(8,128)(2,1)} %get-tuple-element.25.hidden, f32[8,320]{1,0:T(8,128)} %add.125.stats, f32[1,320]{1,0:T(1,128)} %reshape.36.gain, f32[1,320]{1,0:T(1,128)} %reshape.37.shift), custom_call_target="tpu_custom_call" | custom-call | tf_op jit(solution)/shard_map/pallas_call | solution.py:499
  110.7 5.2 %shard_map.117 = (bf16[16,128,320]{2,1,0:T(8,128)(2,1)}, bf16[1,128,320]{2,1,0:T(8,128)(2,1)}, bf16[1,128,320]{2,1,0:T(8,128)(2,1)}, bf16[1,16,320]{2,1,0:T(8,128)(2,1)}, bf16[1,16,320]{2,1,0:T(8,128)(2,1)}) custom-call(f32[2048,320]{1,0:T(8,128)} %get-tuple-element.27.grad_pre, bf16[2048,320]{1,0:T(8,128)(2,1)} %get-tuple-element.25.hidden, ...), custom_call_target="tpu_custom_call" | custom-call | tf_op jit(solution)/shard_map/pallas_call | solution.py:517
  115.9 13.2 %shard_map.123 = f32[3072,320]{1,0:T(8,128)} custom-call(s32[4]{0:T(128)} %add_convert_fusion.flags, s32[64]{0:T(128)} %fusion.10.places, bf16[16,128,320]{2,1,0:T(8,128)(2,1)} %bitcast.66, bf16[128,320]{1,0:T(8,128)(2,1)} %get-tuple-element.70.top, bf16[128,320]{1,0:T(8,128)(2,1)} %get-tuple-element.68.bottom, bf16[24,320]{1,0:T(8,128)(2,1)} %get-tuple-element.82.left, ...), custom_call_target="tpu_custom_call" | custom-call | tf_op jit(solution)/shard_map/pallas_call | solution.py:523
  149.8 3.3 collective-permute-done.14.below
  155.3 3.7 %collective-permute-start.15 = (bf16[1,24,320]{2,1,0:T(8,128)(2,1)}, bf16[1,24,320]{2,1,0:T(8,128)(2,1)S(1)}, u32[]{:S(2)}, u32[]{:S(2)}) collective-permute-start(bf16[1,24,320]{2,1,0:T(8,128)(2,1)} %shard_map.118), channel_id=1, source_target_pairs={{0,1},{2,3},{4,5},{6,7},{8,9},{10,11},{12,13},{14,15},{16,17},{18,... | collective-permute-start | bytes 46088 | tf_op jit(solution)/shard_map/ppermute | solution.py:356
  161.9 4.5 %collective-permute-done.16 = bf16[1,24,320]{2,1,0:T(8,128)(2,1)S(1)} collective-permute-done((bf16[1,24,320]{2,1,0:T(8,128)(2,1)}, bf16[1,24,320]{2,1,0:T(8,128)(2,1)S(1)}, u32[]{:S(2)}, u32[]{:S(2)}) %collective-permute-start.16) | collective-permute-done | bytes 15392 | tf_op jit(solution)/shard_map/ppermute | solution.py:356
  167.0 13.9 %shard_map.120.grad = f32[2048,320]{1,0:T(8,128)} custom-call(s32[4]{0:T(128)} %add_convert_fusion.flags, bf16[16,128,320]{2,1,0:T(8,128)(2,1)} %get-tuple-element.29.core.grad_hidden, bf16[128,320]{1,0:T(8,128)(2,1)} %bitcast.79, bf16[128,320]{1,0:T(8,128)(2,1)} %bitcast.80, bf16[24,320]{1,0:T(8,128)(2,1)} %bitcast.81, bf16[24,320]{1,0:T(8,128)(2,1)} %bitcast.82, ...), custom_call_target="tpu_custom_call" | custom-call | tf_op jit(solution)/shard_map/pallas_call | solution.py:528
  180.9 6.7 %shard_map.121 = (f32[2048,320]{1,0:T(8,128)}, f32[8,320]{1,0:T(8,128)}) custom-call(f32[2048,320]{1,0:T(8,128)} %shard_map.120.grad, bf16[2048,320]{1,0:T(8,128)(2,1)} %bitcast.67, f32[8,320]{1,0:T(8,128)} %add.122.stats, f32[1,320]{1,0:T(1,128)} %reshape.34.gain, f32[1,320]{1,0:T(1,128)} %reshape.35.shift), custom_call_target="tpu_custom_call" | custom-call | tf_op jit(solution)/shard_map/pallas_call | solution.py:529
  187.6 8.7 %collective-permute-start.17 = (f32[8,320]{1,0:T(8,128)}, f32[8,320]{1,0:T(8,128)S(1)}, u32[]{:S(2)}, u32[]{:S(2)}) collective-permute-start(f32[8,320]{1,0:T(8,128)} %get-tuple-element.35), channel_id=1, source_target_pairs={{0,2},{2,0},{4,6},{6,4},{1,3},{3,1},{5,7},{7,5},{8,10},{10,8},{12,... | collective-permute-start | bytes 30728 | tf_op jit(solution)/shard_map/ppermute | solution.py:337
  198.1 3.7 %collective-permute-start.18 = (f32[8,320]{1,0:T(8,128)S(1)}, f32[8,320]{1,0:T(8,128)}, u32[]{:S(2)}, u32[]{:S(2)}) collective-permute-start(f32[8,320]{1,0:T(8,128)S(1)} %add.129), channel_id=1, source_target_pairs={{0,4},{2,6},{4,0},{6,2},{1,5},{3,7},{5,1},{7,3},{8,12},{10,14},{12... | collective-permute-start | bytes 30728 | tf_op jit(solution)/shard_map/ppermute | solution.py:337
  217.6 15.1 %collective-permute-done.22 = f32[192,320]{1,0:T(8,128)S(1)} collective-permute-done((f32[192,320]{1,0:T(8,128)S(1)}, f32[192,320]{1,0:T(8,128)S(1)}, u32[]{:S(2)}, u32[]{:S(2)}) %collective-permute-start.22) | collective-permute-done | bytes 245792 | tf_op jit(solution)/shard_map/ppermute | solution.py:337
  237.0 5.2 %collective-permute-done.23 = f32[384,320]{0,1:T(8,128)} collective-permute-done((f32[384,320]{0,1:T(8,128)}, f32[384,320]{0,1:T(8,128)}, u32[]{:S(2)}, u32[]{:S(2)}) %collective-permute-start.23) | collective-permute-done | bytes 491552 | tf_op jit(solution)/shard_map/ppermute | solution.py:337
  246.7 5.9 %collective-permute-done.24 = f32[192,320]{1,0:T(8,128)S(1)} collective-permute-done((f32[192,320]{1,0:T(8,128)S(1)}, f32[192,320]{1,0:T(8,128)S(1)}, u32[]{:S(2)}, u32[]{:S(2)}) %collective-permute-start.24) | collective-permute-done | bytes 245792 | tf_op jit(solution)/shard_map/ppermute | solution.py:337
  255.7 2.7 collective-permute-start.40
  258.4 5.4 %collective-permute-done.25 = f32[2,96,320]{2,1,0:T(8,128)S(1)} collective-permute-done((f32[2,96,320]{2,1,0:T(8,128)S(1)}, f32[2,96,320]{2,1,0:T(8,128)S(1)}, u32[]{:S(2)}, u32[]{:S(2)}) %collective-permute-start.25) | collective-permute-done | bytes 245792 | tf_op jit(solution)/shard_map/ppermute | solution.py:337
  264.9 2.9 collective-permute-done.40
  267.9 5.3 %collective-permute-done.26 = f32[2,48,320]{2,1,0:T(8,128)S(1)} collective-permute-done((f32[2,48,320]{2,1,0:T(8,128)S(1)}, f32[2,48,320]{2,1,0:T(8,128)S(1)}, u32[]{:S(2)}, u32[]{:S(2)}) %collective-permute-start.26) | collective-permute-done | bytes 122912 | tf_op jit(solution)/shard_map/ppermute | solution.py:337
  279.5 2.7 collective-permute-done.42
  309.5 2.4 copy.25
  312.5 3.6 %collective-permute-done.48 = f32[4,320]{1,0:T(4,128)S(1)} collective-permute-done((f32[4,320]{1,0:T(4,128)S(1)}, f32[4,320]{1,0:T(4,128)S(1)}, u32[]{:S(2)}, u32[]{:S(2)}) %collective-permute-start.48) | collective-permute-done | bytes 5152 | tf_op jit(solution)/shard_map/ppermute | solution.py:337
  317.1 5.8 %shard_map.122 = bf16[16,128,320]{2,1,0:T(8,128)(2,1)} custom-call(f32[2048,320]{1,0:T(8,128)} %get-tuple-element.34.grad_pre, bf16[16,128,320]{2,1,0:T(8,128)(2,1)} %bitcast.68, bf16[16,128,320]{2,1,0:T(8,128)(2,1)} %bitcast.72, f32[8,320]{1,0:T(8,128)} %add.122.stats, f32[8,320]{1,0:T(8,128)} %copy-done.10, f32[1,320]{1,0:T(1,128)} %reshape.34.gain), custom_call_target="tpu_custom_call" | custom-call | tf_op jit(solution)/shard_map/pallas_call | solution.py:533
  322.9 2.5 copy.35
  328.9 4.4 %shard_map.126 = f32[2880,320]{1,0:T(8,128)} custom-call(s32[64]{0:T(128)} %fusion.10.places, bf16[3072,320]{1,0:T(8,128)(2,1)} %constant_dynamic-update-slice_fusion.19.mine), custom_call_target="tpu_custom_call" | custom-call | tf_op jit(solution)/shard_map/pallas_call | solution.py:548
  336.5 4.4 %shard_map.124 = f32[2880,320]{1,0:T(8,128)} custom-call(s32[64]{0:T(128)} %fusion.10.places, bf16[3072,320]{1,0:T(8,128)(2,1)} %copy-done.3), custom_call_target="tpu_custom_call" | custom-call | tf_op jit(solution)/shard_map/pallas_call | solution.py:548
  (222 shorter events, 146.8 us)
Async XLA Ops:
  8.6 16.9 %collective-permute-start = (bf16[2,128,320]{2,1,0:T(8,128)(2,1)}, bf16[2,128,320]{2,1,0:T(8,128)(2,1)S(1)}, u32[]{:S(2)}, u32[]{:S(2)}) collective-permute-start(bf16[2,128,320]{2,1,0:T(8,128)(2,1)} %get-tuple-element.20), channel_id=1, source_target_pairs={{0,2},{2,4},{4,6},{1,3},{3,5},{5,7},{8,10},{10,12},{12,14},{9,11},... | collective-permute-start | bytes 491528 | tf_op jit(solution)/shard_map/ppermute | solution.py:356
  11.0 14.5 %collective-permute-start.1 = (bf16[2,128,320]{2,1,0:T(8,128)(2,1)}, bf16[2,128,320]{2,1,0:T(8,128)(2,1)S(1)}, u32[]{:S(2)}, u32[]{:S(2)}) collective-permute-start(bf16[2,128,320]{2,1,0:T(8,128)(2,1)} %get-tuple-element.21), channel_id=1, source_target_pairs={{2,0},{4,2},{6,4},{3,1},{5,3},{7,5},{10,8},{12,10},{14,12},{11,9},... | collective-permute-start | bytes 491528 | tf_op jit(solution)/shard_map/ppermute | solution.py:356
  28.0 9.7 %collective-permute-start.2 = (bf16[2,24,320]{2,1,0:T(8,128)(2,1)}, bf16[2,24,320]{2,1,0:T(8,128)(2,1)S(1)}, u32[]{:S(2)}, u32[]{:S(2)}) collective-permute-start(bf16[2,24,320]{2,1,0:T(8,128)(2,1)} %shard_map.112), channel_id=1, source_target_pairs={{0,1},{2,3},{4,5},{6,7},{8,9},{10,11},{12,13},{14,15},{16,17},{18,... | collective-permute-start | bytes 92168 | tf_op jit(solution)/shard_map/ppermute | solution.py:356
  80.3 52.3 %collective-permute-start.34 = (f32[1536,320]{0,1:T(8,128)}, f32[1536,320]{0,1:T(8,128)}, u32[]{:S(2)}, u32[]{:S(2)}) collective-permute-start(f32[1536,320]{0,1:T(8,128)} %copy.27), channel_id=1, source_target_pairs={{0,2},{2,0},{4,6},{6,4},{1,3},{3,1},{5,7},{7,5},{8,10},{10,8},{12,... | collective-permute-start | bytes 5898248 | tf_op jit(solution)/shard_map/ppermute | solution.py:337
  132.6 7.4 %collective-permute-start.20 = (f32[1536,320]{0,1:T(8,128)}, f32[1536,320]{0,1:T(8,128)}, u32[]{:S(2)}, u32[]{:S(2)}) collective-permute-start(f32[1536,320]{0,1:T(8,128)} %copy.19), channel_id=1, source_target_pairs={{0,2},{2,0},{4,6},{6,4},{1,3},{3,1},{5,7},{7,5},{8,10},{10,8},{12,... | collective-permute-start | bytes 5898248 | tf_op jit(solution)/shard_map/ppermute | solution.py:337
  138.1 63.7 %collective-permute-start.35 = (f32[384,320]{0,1:T(8,128)S(1)}, f32[384,320]{0,1:T(8,128)S(1)}, u32[]{:S(2)}, u32[]{:S(2)}) collective-permute-start(f32[384,320]{0,1:T(8,128)S(1)} %copy.29), channel_id=1, source_target_pairs={{0,4},{2,6},{4,0},{6,2},{1,5},{3,7},{5,1},{7,3},{8,12},{10,14},{12... | collective-permute-start | bytes 1474568 | tf_op jit(solution)/shard_map/ppermute | solution.py:337
  146.3 61.5 %collective-permute-start.21 = (f32[384,320]{0,1:T(8,128)}, f32[384,320]{0,1:T(8,128)}, u32[]{:S(2)}, u32[]{:S(2)}) collective-permute-start(f32[384,320]{0,1:T(8,128)} %copy.21), channel_id=1, source_target_pairs={{0,4},{2,6},{4,0},{6,2},{1,5},{3,7},{5,1},{7,3},{8,12},{10,14},{12... | collective-permute-start | bytes 1474568 | tf_op jit(solution)/shard_map/ppermute | solution.py:337
  155.3 6.6 %collective-permute-start.15 = (bf16[1,24,320]{2,1,0:T(8,128)(2,1)}, bf16[1,24,320]{2,1,0:T(8,128)(2,1)S(1)}, u32[]{:S(2)}, u32[]{:S(2)}) collective-permute-start(bf16[1,24,320]{2,1,0:T(8,128)(2,1)} %shard_map.118), channel_id=1, source_target_pairs={{0,1},{2,3},{4,5},{6,7},{8,9},{10,11},{12,13},{14,15},{16,17},{18,... | collective-permute-start | bytes 46088 | tf_op jit(solution)/shard_map/ppermute | solution.py:356
  187.6 9.8 %collective-permute-start.17 = (f32[8,320]{1,0:T(8,128)}, f32[8,320]{1,0:T(8,128)S(1)}, u32[]{:S(2)}, u32[]{:S(2)}) collective-permute-start(f32[8,320]{1,0:T(8,128)} %get-tuple-element.35), channel_id=1, source_target_pairs={{0,2},{2,0},{4,6},{6,4},{1,3},{3,1},{5,7},{7,5},{8,10},{10,8},{12,... | collective-permute-start | bytes 30728 | tf_op jit(solution)/shard_map/ppermute | solution.py:337
  198.1 56.3 %collective-permute-start.18 = (f32[8,320]{1,0:T(8,128)S(1)}, f32[8,320]{1,0:T(8,128)}, u32[]{:S(2)}, u32[]{:S(2)}) collective-permute-start(f32[8,320]{1,0:T(8,128)S(1)} %add.129), channel_id=1, source_target_pairs={{0,4},{2,6},{4,0},{6,2},{1,5},{3,7},{5,1},{7,3},{8,12},{10,14},{12... | collective-permute-start | bytes 30728 | tf_op jit(solution)/shard_map/ppermute | solution.py:337
  205.7 10.8 %collective-permute-start.36 = (f32[192,320]{1,0:T(8,128)}, f32[192,320]{1,0:T(8,128)}, u32[]{:S(2)}, u32[]{:S(2)}) collective-permute-start(f32[192,320]{1,0:T(8,128)} %slice.217), channel_id=1, source_target_pairs={{0,1},{1,0},{2,3},{3,2},{4,5},{5,4},{6,7},{7,6},{8,9},{9,8},{10,11... | collective-permute-start | bytes 737288 | tf_op jit(solution)/shard_map/ppermute | solution.py:337
  205.7 27.9 %collective-permute-start.37 = (f32[384,320]{0,1:T(8,128)}, f32[384,320]{0,1:T(8,128)}, u32[]{:S(2)}, u32[]{:S(2)}) collective-permute-start(f32[384,320]{0,1:T(8,128)} %copy.31), channel_id=1, source_target_pairs={{0,1},{1,0},{2,3},{3,2},{4,5},{5,4},{6,7},{7,6},{8,9},{9,8},{10,11... | collective-permute-start | bytes 1474568 | tf_op jit(solution)/shard_map/ppermute | solution.py:337
  214.5 18.2 %collective-permute-start.22 = (f32[192,320]{1,0:T(8,128)S(1)}, f32[192,320]{1,0:T(8,128)S(1)}, u32[]{:S(2)}, u32[]{:S(2)}) collective-permute-start(f32[192,320]{1,0:T(8,128)S(1)} %slice.201), channel_id=1, source_target_pairs={{0,1},{1,0},{2,3},{3,2},{4,5},{5,4},{6,7},{7,6},{8,9},{9,8},{10,11... | collective-permute-start | bytes 737288 | tf_op jit(solution)/shard_map/ppermute | solution.py:337
  214.6 27.7 %collective-permute-start.23 = (f32[384,320]{0,1:T(8,128)}, f32[384,320]{0,1:T(8,128)}, u32[]{:S(2)}, u32[]{:S(2)}) collective-permute-start(f32[384,320]{0,1:T(8,128)} %copy.23), channel_id=1, source_target_pairs={{0,1},{1,0},{2,3},{3,2},{4,5},{5,4},{6,7},{7,6},{8,9},{9,8},{10,11... | collective-permute-start | bytes 1474568 | tf_op jit(solution)/shard_map/ppermute | solution.py:337
  236.9 8.1 %collective-permute-start.38 = (f32[192,320]{1,0:T(8,128)S(1)}, f32[192,320]{1,0:T(8,128)S(1)}, u32[]{:S(2)}, u32[]{:S(2)}) collective-permute-start(f32[192,320]{1,0:T(8,128)S(1)} %slice.221), channel_id=1, source_target_pairs={{0,4},{2,6},{4,0},{6,2},{1,5},{3,7},{5,1},{7,3},{8,12},{10,14},{12... | collective-permute-start | bytes 737288 | tf_op jit(solution)/shard_map/ppermute | solution.py:337
  244.7 8.0 %collective-permute-start.24 = (f32[192,320]{1,0:T(8,128)S(1)}, f32[192,320]{1,0:T(8,128)S(1)}, u32[]{:S(2)}, u32[]{:S(2)}) collective-permute-start(f32[192,320]{1,0:T(8,128)S(1)} %slice.205), channel_id=1, source_target_pairs={{0,4},{2,6},{4,0},{6,2},{1,5},{3,7},{5,1},{7,3},{8,12},{10,14},{12... | collective-permute-start | bytes 737288 | tf_op jit(solution)/shard_map/ppermute | solution.py:337
  245.1 10.6 %collective-permute-start.39 = (f32[2,96,320]{2,1,0:T(8,128)S(1)}, f32[2,96,320]{2,1,0:T(8,128)S(1)}, u32[]{:S(2)}, u32[]{:S(2)}) collective-permute-start(f32[2,96,320]{2,1,0:T(8,128)S(1)} %pad_maximum_fusion), channel_id=1, source_target_pairs={{0,8},{8,0},{16,24},{24,16},{1,9},{9,1},{17,25},{25,17},{2,10},{10... | collective-permute-start | bytes 737288 | tf_op jit(solution)/shard_map/ppermute | solution.py:337
  252.7 11.0 %collective-permute-start.25 = (f32[2,96,320]{2,1,0:T(8,128)S(1)}, f32[2,96,320]{2,1,0:T(8,128)S(1)}, u32[]{:S(2)}, u32[]{:S(2)}) collective-permute-start(f32[2,96,320]{2,1,0:T(8,128)S(1)} %pad_maximum_fusion.1), channel_id=1, source_target_pairs={{0,8},{8,0},{16,24},{24,16},{1,9},{9,1},{17,25},{25,17},{2,10},{10... | collective-permute-start | bytes 737288 | tf_op jit(solution)/shard_map/ppermute | solution.py:337
  255.1 23.1 %collective-permute-start.19 = (f32[8,320]{1,0:T(8,128)S(1)}, f32[8,320]{1,0:T(8,128)S(1)}, u32[]{:S(2)}, u32[]{:S(2)}) collective-permute-start(f32[8,320]{1,0:T(8,128)S(1)} %add.130), channel_id=1, source_target_pairs={{0,1},{1,0},{2,3},{3,2},{4,5},{5,4},{6,7},{7,6},{8,9},{9,8},{10,11... | collective-permute-start | bytes 30728 | tf_op jit(solution)/shard_map/ppermute | solution.py:337
  255.7 12.1 %collective-permute-start.40 = (f32[2,48,320]{2,1,0:T(8,128)S(1)}, f32[2,48,320]{2,1,0:T(8,128)S(1)}, u32[]{:S(2)}, u32[]{:S(2)}) collective-permute-start(f32[2,48,320]{2,1,0:T(8,128)S(1)} %slice.225), channel_id=1, source_target_pairs={{0,16},{8,24},{16,0},{24,8},{1,17},{9,25},{17,1},{25,9},{2,18},{10... | collective-permute-start | bytes 368648 | tf_op jit(solution)/shard_map/ppermute | solution.py:337
  263.8 9.4 %collective-permute-start.26 = (f32[2,48,320]{2,1,0:T(8,128)S(1)}, f32[2,48,320]{2,1,0:T(8,128)S(1)}, u32[]{:S(2)}, u32[]{:S(2)}) collective-permute-start(f32[2,48,320]{2,1,0:T(8,128)S(1)} %slice.209), channel_id=1, source_target_pairs={{0,16},{8,24},{16,0},{24,8},{1,17},{9,25},{17,1},{25,9},{2,18},{10... | collective-permute-start | bytes 368648 | tf_op jit(solution)/shard_map/ppermute | solution.py:337
  267.8 7.7 %collective-permute-start.41 = (bf16[2,48,320]{2,1,0:T(8,128)(2,1)S(1)}, bf16[2,48,320]{2,1,0:T(8,128)(2,1)S(1)}, u32[]{:S(2)}, u32[]{:S(2)}) collective-permute-start(bf16[2,48,320]{2,1,0:T(8,128)(2,1)S(1)} %fusion.8), channel_id=1, source_target_pairs={{0,16},{8,24},{16,0},{24,8},{1,17},{9,25},{17,1},{25,9},{2,18},{10... | collective-permute-start | bytes 184328 | tf_op jit(solution)/shard_map/ppermute | solution.py:337
  275.5 6.6 %collective-permute-start.42 = (bf16[2,96,320]{2,1,0:T(8,128)(2,1)S(1)}, bf16[2,96,320]{2,1,0:T(8,128)(2,1)S(1)}, u32[]{:S(2)}, u32[]{:S(2)}) collective-permute-start(bf16[2,96,320]{2,1,0:T(8,128)(2,1)S(1)} %pad_maximum_fusion.9), channel_id=1, source_target_pairs={{0,8},{8,0},{16,24},{24,16},{1,9},{9,1},{17,25},{25,17},{2,10},{10... | collective-permute-start | bytes 368648 | tf_op jit(solution)/shard_map/ppermute | solution.py:337
  282.3 8.9 %collective-permute-start.45 = (bf16[192,320]{1,0:T(8,128)(2,1)S(1)}, bf16[192,320]{1,0:T(8,128)(2,1)S(1)}, u32[]{:S(2)}, u32[]{:S(2)}) collective-permute-start(bf16[192,320]{1,0:T(8,128)(2,1)S(1)} %get-tuple-element.56), channel_id=1, source_target_pairs={{0,4},{2,6},{4,0},{6,2},{1,5},{3,7},{5,1},{7,3},{8,12},{10,14},{12... | collective-permute-start | bytes 368648 | tf_op jit(solution)/shard_map/ppermute | solution.py:337
  285.8 9.5 %collective-permute-start.31 = (bf16[192,320]{1,0:T(8,128)(2,1)S(1)}, bf16[192,320]{1,0:T(8,128)(2,1)S(1)}, u32[]{:S(2)}, u32[]{:S(2)}) collective-permute-start(bf16[192,320]{1,0:T(8,128)(2,1)S(1)} %get-tuple-element.66), channel_id=1, source_target_pairs={{0,4},{2,6},{4,0},{6,2},{1,5},{3,7},{5,1},{7,3},{8,12},{10,14},{12... | collective-permute-start | bytes 368648 | tf_op jit(solution)/shard_map/ppermute | solution.py:337
  288.8 10.2 %collective-permute-start.44 = (bf16[384,320]{1,0:T(8,128)(2,1)S(1)}, bf16[384,320]{1,0:T(8,128)(2,1)S(1)}, u32[]{:S(2)}, u32[]{:S(2)}) collective-permute-start(bf16[384,320]{1,0:T(8,128)(2,1)S(1)} %pad_maximum_fusion.6), channel_id=1, source_target_pairs={{0,4},{2,6},{4,0},{6,2},{1,5},{3,7},{5,1},{7,3},{8,12},{10,14},{12... | collective-permute-start | bytes 737288 | tf_op jit(solution)/shard_map/ppermute | solution.py:337
  291.2 10.2 %collective-permute-start.46 = (bf16[384,320]{1,0:T(8,128)(2,1)S(1)}, bf16[384,320]{1,0:T(8,128)(2,1)S(1)}, u32[]{:S(2)}, u32[]{:S(2)}) collective-permute-start(bf16[384,320]{1,0:T(8,128)(2,1)S(1)} %pad_maximum_fusion.7), channel_id=1, source_target_pairs={{0,1},{1,0},{2,3},{3,2},{4,5},{5,4},{6,7},{7,6},{8,9},{9,8},{10,11... | collective-permute-start | bytes 737288 | tf_op jit(solution)/shard_map/ppermute | solution.py:337
  294.7 9.9 %collective-permute-start.30 = (bf16[384,320]{1,0:T(8,128)(2,1)}, bf16[384,320]{1,0:T(8,128)(2,1)}, u32[]{:S(2)}, u32[]{:S(2)}) collective-permute-start(bf16[384,320]{1,0:T(8,128)(2,1)} %pad_maximum_fusion.3), channel_id=1, source_target_pairs={{0,4},{2,6},{4,0},{6,2},{1,5},{3,7},{5,1},{7,3},{8,12},{10,14},{12... | collective-permute-start | bytes 737288 | tf_op jit(solution)/shard_map/ppermute | solution.py:337
  296.1 11.6 %collective-permute-start.32 = (bf16[384,320]{1,0:T(8,128)(2,1)}, bf16[384,320]{1,0:T(8,128)(2,1)}, u32[]{:S(2)}, u32[]{:S(2)}) collective-permute-start(bf16[384,320]{1,0:T(8,128)(2,1)} %pad_maximum_fusion.4), channel_id=1, source_target_pairs={{0,1},{1,0},{2,3},{3,2},{4,5},{5,4},{6,7},{7,6},{8,9},{9,8},{10,11... | collective-permute-start | bytes 737288 | tf_op jit(solution)/shard_map/ppermute | solution.py:337
  304.6 21.5 %collective-permute-start.47 = (bf16[1536,320]{0,1:T(8,128)(2,1)}, bf16[1536,320]{0,1:T(8,128)(2,1)}, u32[]{:S(2)}, u32[]{:S(2)}) collective-permute-start(bf16[1536,320]{0,1:T(8,128)(2,1)} %copy.33), channel_id=1, source_target_pairs={{0,2},{2,0},{4,6},{6,4},{1,3},{3,1},{5,7},{7,5},{8,10},{10,8},{12,... | collective-permute-start | bytes 2949128 | tf_op jit(solution)/shard_map/ppermute | solution.py:337
  311.8 21.4 %collective-permute-start.33 = (bf16[1536,320]{0,1:T(8,128)(2,1)}, bf16[1536,320]{0,1:T(8,128)(2,1)}, u32[]{:S(2)}, u32[]{:S(2)}) collective-permute-start(bf16[1536,320]{0,1:T(8,128)(2,1)} %copy.25), channel_id=1, source_target_pairs={{0,2},{2,0},{4,6},{6,4},{1,3},{3,1},{5,7},{7,5},{8,10},{10,8},{12,... | collective-permute-start | bytes 2949128 | tf_op jit(solution)/shard_map/ppermute | solution.py:337
  316.1 9.4 %collective-permute-start.49 = (f32[4,320]{1,0:T(4,128)S(1)}, f32[4,320]{1,0:T(4,128)S(1)}, u32[]{:S(2)}, u32[]{:S(2)}) collective-permute-start(f32[4,320]{1,0:T(4,128)S(1)} %fusion.11), channel_id=1, source_target_pairs={{0,16},{8,24},{16,0},{24,8},{1,17},{9,25},{17,1},{25,9},{2,18},{10... | collective-permute-start | bytes 15368 | tf_op jit(solution)/shard_map/ppermute | solution.py:337
  (40 other events, 269.8 us)

commit v2 on v1

v2 whole, which is shorter than its diff:
```python
import functools

import jax
import jax.numpy as jnp
from jax import lax
from jax.experimental import pallas as pl
from jax.experimental.pallas import tpu as pltpu
from jax.sharding import PartitionSpec as P

GROUPS = 32
EPS = 1e-05
F32 = jnp.float32
BF16 = jnp.bfloat16
CHUNK = 4
LANES = 128
LIMIT = 24 * 2**20
VMEM = pl.BlockSpec(memory_space=pltpu.VMEM)
SMEM = pl.BlockSpec(memory_space=pltpu.SMEM)


def call(body, out_shape, n_in, scratch=(), smem=0):
    return pl.pallas_call(
        body,
        out_shape=out_shape,
        in_specs=[SMEM] * smem + [VMEM] * n_in,
        out_specs=jax.tree.map(lambda _: VMEM, out_shape),
        scratch_shapes=list(scratch),
        compiler_params=pltpu.CompilerParams(vmem_limit_bytes=LIMIT),
    )


def shape(dims, dtype):
    return jax.ShapeDtypeStruct(dims, dtype)


def group_total(rows):
    chans = rows.shape[1]
    width = chans // GROUPS
    left = lax.broadcasted_iota(jnp.int32, (chans, chans), 0).astype(F32)
    right = lax.broadcasted_iota(jnp.int32, (chans, chans), 1).astype(F32)
    same = jnp.floor((left + 0.5) / width) == jnp.floor((right + 0.5) / width)
    return jnp.dot(
        rows,
        same.astype(F32),
        precision=lax.Precision.HIGHEST,
        preferred_element_type=F32,
    )


def mean_rstd(stats_a, stats_b, count):
    total = group_total(stats_a[...] + stats_b[...])
    mean = total[0:1] / count
    spread = total[1:2] / count - mean * mean
    return mean, lax.rsqrt(spread + EPS)


def silu(pre):
    return pre / (1.0 + jnp.exp(-pre))


def silu_slope(pre):
    sigma = 1.0 / (1.0 + jnp.exp(-pre))
    return sigma * (1.0 + pre * (1.0 - sigma))


def pair_rows(first, second):
    rows = lax.broadcasted_iota(jnp.int32, (8, first.shape[1]), 0)
    first = jnp.sum(first, axis=0, keepdims=True)
    second = jnp.sum(second, axis=0, keepdims=True)
    return jnp.where(rows == 0, first, jnp.where(rows == 1, second, 0.0))


def fold(block):
    return jnp.sum(block.reshape(block.shape[0] // 8, 8, block.shape[1]), axis=0)


def build_taps(flags, core, halo, which, taps, line, sides, act):
    high, wide, chans = core.shape
    top, bottom, left, right = (part.at[which] for part in halo)
    has_top, has_bottom = flags[0] > 0, flags[1] > 0
    has_left, has_right = flags[2] > 0, flags[3] > 0
    index = lax.broadcasted_iota(jnp.int32, (sides.shape[1], 1), 0)
    inside = ((index > 0) | has_top) & ((index < high + 1) | has_bottom) & (index < high + 2)
    sides[0] = jnp.where(inside & has_left, act(left[...].astype(F32)), 0.0)
    sides[1] = jnp.where(inside & has_right, act(right[...].astype(F32)), 0.0)

    def put(position, cells):
        line[7:8, :] = sides[0, pl.ds(position, 1), :]
        line[8 : 8 + wide, :] = cells
        line[8 + wide : 9 + wide, :] = sides[1, pl.ds(position, 1), :]
        for tap in range(3):
            taps[position, :, tap * chans : (tap + 1) * chans] = line[
                7 + tap : 7 + tap + wide, :
            ].astype(BF16)

    put(0, jnp.where(has_top, act(top[...].astype(F32)), 0.0))
    put(high + 1, jnp.where(has_bottom, act(bottom[...].astype(F32)), 0.0))

    def step(row, carry):
        put(row + 1, act(core[row].astype(F32)))
        return carry

    lax.fori_loop(0, high, step, 0)


def flip_weights(kernel, turned):
    chans = turned.shape[1]
    for across in range(3):
        for along in range(3):
            tap = 3 * (2 - across) + 2 - along
            turned[across, :, along * chans : (along + 1) * chans] = kernel[
                tap * chans : (tap + 1) * chans, :
            ]


def conv_rows(taps, weight, first, rows, turned):
    wide, depth = taps.shape[1], taps.shape[2]
    total = None
    for across in range(3):
        cells = taps[pl.ds(first + across, rows)].reshape(rows * wide, depth)
        dims = (((1,), (1 if turned else 0,)), ((), ()))
        part = lax.dot_general(cells, weight(across), dims, preferred_element_type=F32)
        total = part if total is None else total + part
    return total


def edges_of(array, which, lefts, rights, edge):
    high, wide = array.shape[:2]
    for target, at in ((lefts, 0), (rights, wide - 8)):
        inner = 0 if at == 0 else 7
        for row in range(high):
            strip = array[row, at : at + 8, :].astype(F32)
            edge[row : row + 1, :] = strip[inner : inner + 1, :]
        target[which] = edge[...].astype(BF16)


def identity(cells):
    return cells


def look_kernel(core, upstream, stats, tops, bottoms, lefts, rights, edge):
    high, wide, chans = core.shape

    def step(row, carry):
        cells = core[row].astype(F32)
        return carry[0] + fold(cells), carry[1] + fold(cells * cells)

    zero = jnp.zeros((8, chans), F32)
    stats[...] = pair_rows(*lax.fori_loop(0, high, step, (zero, zero)))
    for which, array in enumerate((core, upstream)):
        tops[which] = array[0]
        bottoms[which] = array[high - 1]
        edges_of(array, which, lefts, rights, edge)


def sides_kernel(flags, lefts, rights, above, below, *refs):
    outs, line = refs[:-1], refs[-1]
    count, high, chans = lefts.shape
    wide = above.shape[1]

    def column(which, edges, at):
        inner = 0 if at == 0 else 7
        line[0:1, :] = above[which, at : at + 8, :].astype(F32)[inner : inner + 1, :]
        line[1 : 1 + high, :] = edges[which].astype(F32)
        line[1 + high : 2 + high, :] = below[which, at : at + 8, :].astype(F32)[
            inner : inner + 1, :
        ]
        return line[...]

    line[...] = jnp.zeros_like(line)
    for which in range(count):
        last = column(which, rights, wide - 8)
        first = column(which, lefts, 0)
        if len(outs) == 1:
            outs[0][which] = jnp.where(flags[3] > 0, last, first).astype(BF16)
        else:
            outs[0][which] = last.astype(BF16)
            outs[1][which] = first.astype(BF16)


def hidden_kernel(
    flags, core, top, bottom, left, right, kernel, stats_a, stats_b, gain, shift,
    hidden, sums, taps, line, sides, *, count,
):
    high, wide, chans = core.shape
    mean, rstd = mean_rstd(stats_a, stats_b, count)
    scale = rstd * gain[...]
    offset = shift[...] - mean * scale
    build_taps(
        flags, core, (top, bottom, left, right), 0, taps, line, sides,
        lambda cells: silu(cells * scale + offset),
    )
    depth = taps.shape[2]

    def step(index, carry):
        block = conv_rows(
            taps,
            lambda across: kernel[across * depth : (across + 1) * depth, :],
            index * CHUNK, CHUNK, False,
        ).astype(BF16)
        hidden[pl.ds(index * CHUNK * wide, CHUNK * wide), :] = block
        wideb = block.astype(F32)
        return carry[0] + fold(wideb), carry[1] + fold(wideb * wideb)

    zero = jnp.zeros((8, chans), F32)
    sums[...] = pair_rows(*lax.fori_loop(0, high // CHUNK, step, (zero, zero)))


def back_conv_kernel(
    flags, core, top, bottom, left, right, kernel, source, stats_a, stats_b, gain, shift,
    out, sums, taps, line, sides, turned, *, count, which,
):
    high, wide, chans = core.shape
    mean, rstd = mean_rstd(stats_a, stats_b, count)
    build_taps(flags, core, (top, bottom, left, right), which, taps, line, sides, identity)
    flip_weights(kernel, turned)

    def step(index, carry):
        window = pl.ds(index * CHUNK * wide, CHUNK * wide)
        grad = conv_rows(taps, lambda across: turned[across], index * CHUNK, CHUNK, True)
        normal = (source[window, :].astype(F32) - mean) * rstd
        block = grad * silu_slope(normal * gain[...] + shift[...])
        out[window, :] = block
        return carry[0] + fold(block), carry[1] + fold(block * normal)

    zero = jnp.zeros((8, chans), F32)
    sums[...] = pair_rows(*lax.fori_loop(0, high // CHUNK, step, (zero, zero)))


def norm_back_terms(stats_a, stats_b, sums_a, sums_b, gain, count):
    mean, rstd = mean_rstd(stats_a, stats_b, count)
    means = group_total((sums_a[...] + sums_b[...]) * gain[...]) / count
    return mean, rstd, means[0:1], means[1:2]


def grad_hidden_kernel(
    grad_pre, hidden, stats_a, stats_b, sums_a, sums_b, gain,
    out, tops, bottoms, lefts, rights, edge, *, count,
):
    mean, rstd, mean_one, mean_two = norm_back_terms(
        stats_a, stats_b, sums_a, sums_b, gain, count
    )
    high, wide, chans = out.shape

    def step(row, carry):
        window = pl.ds(row * wide, wide)
        normal = (hidden[window, :].astype(F32) - mean) * rstd
        block = rstd * (grad_pre[window, :] * gain[...] - mean_one - normal * mean_two)
        out[row] = block.astype(BF16)
        return carry

    lax.fori_loop(0, high, step, 0)
    tops[0] = out[0]
    bottoms[0] = out[high - 1]
    edges_of(out, 0, lefts, rights, edge)


def input_grad_kernel(
    grad_pre, core, upstream, stats_a, stats_b, sums_a, sums_b, gain, out, *, count
):
    mean, rstd, mean_one, mean_two = norm_back_terms(
        stats_a, stats_b, sums_a, sums_b, gain, count
    )
    high, wide, chans = out.shape

    def step(row, carry):
        window = pl.ds(row * wide, wide)
        normal = (core[row].astype(F32) - mean) * rstd
        block = rstd * (grad_pre[window, :] * gain[...] - mean_one - normal * mean_two)
        out[row] = (upstream[row].astype(F32) + block).astype(BF16)
        return carry

    lax.fori_loop(0, high, step, 0)


def scatter_blocks(places, natural, outs, size):
    chans = natural.shape[1]
    whole = chans // LANES
    rest = chans - whole * LANES
    tail = size * rest // LANES
    each = outs[0].shape[0]
    for which, out in enumerate(outs):

        def step(block, carry, which=which, out=out):
            at = pl.multiple_of(places[which * each + block] * size, 8)
            for part in range(whole):
                out[block, part * size : (part + 1) * size, :] = natural[
                    pl.ds(at, size), part * LANES : (part + 1) * LANES
                ]
            for part in range(LANES // rest):
                out[block, whole * size :, part * rest : (part + 1) * rest] = natural[
                    pl.ds(pl.multiple_of(at + part * tail, 8), tail), whole * LANES :
                ]
            return carry

        lax.fori_loop(0, each, step, 0)


def second_grad_kernel(
    flags, places, core, top, bottom, left, right, hidden, stats_a, stats_b, gain, shift,
    keep, send, taps, line, sides, turned, natural, *, count, size,
):
    high, wide, chans = core.shape
    build_taps(flags, core, (top, bottom, left, right), 1, taps, line, sides, identity)
    mean, rstd = mean_rstd(stats_a, stats_b, count)
    scale = rstd * gain[...]
    offset = shift[...] - mean * scale
    depth = taps.shape[2]
    for part in range(high * wide // 256):
        window = slice(part * 256, (part + 1) * 256)
        act = silu(hidden[window, :].astype(F32) * scale + offset)
        turned[:, window] = act.astype(BF16).T
    for across in range(3):
        cells = taps[2 - across : 2 - across + high].reshape(high * wide, depth)
        block = jnp.dot(turned[...], cells, preferred_element_type=F32)
        for along in range(3):
            lanes = slice((2 - along) * chans, (3 - along) * chans)
            first = (3 * across + along) * chans
            natural[first : first + chans, :] = block[:, lanes]
    natural[9 * chans :, :] = jnp.zeros_like(natural[9 * chans :, :])
    scatter_blocks(places, natural, (keep, send), size)


def first_grad_kernel(
    flags, places, core, top, bottom, left, right, grad_hidden, stats_a, stats_b, gain,
    shift, keep, send, taps, line, sides, turned, natural, *, count, size,
):
    high, wide, chans = core.shape
    mean, rstd = mean_rstd(stats_a, stats_b, count)
    scale = rstd * gain[...]
    offset = shift[...] - mean * scale
    build_taps(
        flags, core, (top, bottom, left, right), 0, taps, line, sides,
        lambda cells: silu(cells * scale + offset),
    )
    depth = taps.shape[2]
    rows = 256 // wide
    for part in range(high * wide // 256):
        cells = grad_hidden[part * rows : (part + 1) * rows].reshape(256, chans)
        turned[:, part * 256 : (part + 1) * 256] = cells.T
    for across in range(3):
        cells = taps[across : across + high].reshape(high * wide, depth)
        block = jnp.dot(turned[...], cells, preferred_element_type=F32)
        natural[across * depth : (across + 1) * depth, :] = block.T
    natural[9 * chans :, :] = jnp.zeros_like(natural[9 * chans :, :])
    scatter_blocks(places, natural, (keep, send), size)


def merge_kernel(*refs, terms, layout):
    ins, outs = refs[: -len(layout)], refs[-len(layout) :]
    for out, blocks in zip(outs, layout, strict=True):
        for at, (part, block) in enumerate(blocks):
            total = ins[terms * part][block]
            if terms == 2:
                total = total + ins[2 * part + 1][block]
            out[at] = total.astype(out.dtype)


def spread_kernel(places, mine, other, out, *, size):
    rows, chans = out.shape
    whole = chans // LANES
    rest = chans - whole * LANES
    tail = size * rest // LANES
    each = mine.shape[0]
    for which, source in enumerate((mine, other)):

        def step(block, carry, which=which, source=source):
            place = places[which * each + block]

            @pl.when(place * size < rows)
            def _():
                at = pl.multiple_of(place * size, 8)
                cells = source[block].astype(F32)
                for part in range(whole):
                    out[pl.ds(at, size), part * LANES : (part + 1) * LANES] = cells[
                        part * size : (part + 1) * size
                    ]
                for part in range(LANES // rest):
                    window = pl.ds(pl.multiple_of(at + part * tail, 8), tail)
                    out[window, whole * LANES :] = cells[
                        whole * size :, part * rest : (part + 1) * rest
                    ]

            return carry

        lax.fori_loop(0, each, step, 0)


def swap(value, axis, mask):
    return lax.ppermute(value, axis, [(i, i ^ mask) for i in range(lax.axis_size(axis))])


def bits_of(axis):
    count = lax.axis_size(axis)
    assert count & (count - 1) == 0
    return [(axis, 1 << bit) for bit in range(count.bit_length() - 1)]


def add_up_pair(value, axes):
    *early, (name, mask) = [bit for axis in axes for bit in bits_of(axis)]
    for axis, other in early:
        value = value + swap(value, axis, other)
    return value, swap(value, name, mask)


def shifted(value, axis, step):
    count = lax.axis_size(axis)
    pairs = [(i, i + step) for i in range(count) if 0 <= i + step < count]
    return lax.ppermute(value, axis, pairs)


def borders(flags, tops, bottoms, lefts, rights):
    count, wide, chans = tops.shape
    high = lefts.shape[1]
    above = shifted(bottoms, "row", 1)
    below = shifted(tops, "row", -1)
    pair = lax.axis_size("col") == 2
    out = shape((count, high + 8, chans), BF16)
    sent = call(
        sides_kernel, (out,) if pair else (out, out), 4,
        [pltpu.VMEM((high + 8, chans), F32)], smem=1,
    )(flags, lefts, rights, above, below)
    if pair:
        other = swap(sent[0], "col", 1)
        return above, below, other, other
    return above, below, shifted(sent[0], "col", 1), shifted(sent[1], "col", -1)


def plan():
    row, col, batch = bits_of("row"), bits_of("col"), bits_of("batch")
    return row[:1], row[1:] + col, batch


def exchange_orders():
    first, middle, last = plan()
    return (first + middle + last, first + middle[::-1] + last)


def places_of(blocks):
    half = blocks // 2
    head = len(plan()[0])
    found = []
    for order in exchange_orders():
        own = 0
        for level, (axis, mask) in enumerate(order):
            bit = (lax.axis_index(axis) & mask) // mask
            weight = half >> (level + 1)
            if level < head:
                weight *= 2
            own = own + bit * weight
        found.append(own)
    outer = blocks >> head
    index = jnp.arange(blocks, dtype=jnp.int32)
    chunk = (index % outer) // (outer // 2)
    return index ^ jnp.where(chunk == 0, found[0], found[1])


def merge(parts, layout, dtype=F32):
    terms = len(parts[0])
    tail = parts[0][0].shape[1:]
    return call(
        functools.partial(merge_kernel, terms=terms, layout=layout),
        tuple(shape((len(blocks),) + tail, dtype) for blocks in layout),
        terms * len(parts),
    )(*[array for part in parts for array in part])


def halves(part, first, count):
    blocks = [(part, first + block) for block in range(count)]
    return [blocks[: count // 2], blocks[count // 2 :]]


def give_steps():
    first, middle, last = plan()
    ((axis_one, mask_one),) = first

    def outer(pieces):
        keep, send = pieces
        got = swap(send, axis_one, mask_one)
        count = keep.shape[0]
        layout = halves(0, 0, count // 2) + halves(0, count // 2, count // 2)
        return merge([(keep, got)], layout)

    def chunked(pieces, pair, final):
        got = [swap(pieces[2 * k + 1], axis, mask) for k, (axis, mask) in enumerate(pair)]
        count = pieces[0].shape[0]
        split = [halves(0, 0, count), halves(1, 0, count)]
        layout = split[0] + split[1]
        if final:
            layout = [split[0][k] + split[1][k] for k in range(2)]
        return merge([(pieces[2 * k], got[k]) for k in range(2)], layout)

    def inner(pieces, axis, mask, final):
        got = swap(pieces[1], axis, mask)
        count = pieces[0].shape[0] // 2
        split = [halves(0, 0, count), halves(0, count, count)]
        layout = [split[0][k] + split[1][k] for k in range(2)]
        if final:
            layout = [layout[0] + layout[1]]
        return merge([(pieces[0], got)], layout, BF16 if final else F32)

    steps = [outer]
    pairs = list(zip(middle, middle[::-1], strict=True))
    for level, pair in enumerate(pairs):
        final = level == len(pairs) - 1
        steps.append(functools.partial(chunked, pair=pair, final=final))
    for level, (axis, mask) in enumerate(last):
        final = level == len(last) - 1
        steps.append(functools.partial(inner, axis=axis, mask=mask, final=final))
    return steps


def join(parts, layout):
    return merge([(part,) for part in parts], layout, BF16)


def span(part, count):
    return [(part, block) for block in range(count)]


def take_steps():
    first, middle, last = plan()
    ((axis_one, mask_one),) = first

    def inner(pieces, axis, mask, final):
        (both,) = pieces
        count = both.shape[0]
        blocks = span(0, count) + span(1, count)
        layout = [blocks[0::2], blocks[1::2]] if final else [blocks]
        return join([both, swap(both, axis, mask)], layout)

    def chunked(pieces, pair, final):
        got = [swap(piece, axis, mask) for piece, (axis, mask) in zip(pieces, pair, strict=True)]
        count = pieces[0].shape[0]
        blocks = [span(part, count) for part in range(4)]
        layout = [blocks[0] + blocks[1], blocks[2] + blocks[3]]
        if final:
            layout = [layout[0] + layout[1]]
        return join([pieces[0], got[0], pieces[1], got[1]], layout)

    def outer(pieces):
        return pieces[0], swap(pieces[0], axis_one, mask_one)

    steps = []
    for level, (axis, mask) in enumerate(last[::-1]):
        final = level == len(last) - 1
        steps.append(functools.partial(inner, axis=axis, mask=mask, final=final))
    pairs = list(zip(middle, middle[::-1], strict=True))[::-1]
    for level, pair in enumerate(pairs):
        final = level == len(pairs) - 1
        steps.append(functools.partial(chunked, pair=pair, final=final))
    steps.append(outer)
    return steps


def tie(*values):
    return lax.optimization_barrier(values)


def per_device(
    features, first_kernel, second_kernel, first_gain, first_shift,
    second_gain, second_shift, upstream,
):
    high, wide, chans = features.shape[1:]
    rows, cols = lax.axis_size("row"), lax.axis_size("col")
    devices = rows * cols * lax.axis_size("batch")
    count = float(high * rows * wide * cols * (chans // GROUPS))
    cells = features[0]
    upper = upstream[0]
    weights = [k.reshape(9 * chans, chans) for k in (first_kernel, second_kernel)]
    gains = [g.reshape(1, chans) for g in (first_gain, second_gain)]
    shifts = [s.reshape(1, chans) for s in (first_shift, second_shift)]
    row, col = lax.axis_index("row"), lax.axis_index("col")
    flags = jnp.stack([row > 0, row < rows - 1, col > 0, col < cols - 1]).astype(jnp.int32)
    unit = 2 * devices * 16
    padded = -(-9 * chans // unit) * unit
    blocks = 2 * devices
    size = padded // blocks
    places = places_of(blocks)

    image = shape((high, wide, chans), BF16)
    flat = high * wide
    small = shape((8, chans), F32)
    rows_of = lambda n: shape((n, wide, chans), BF16)
    cols_of = lambda n: shape((n, high, chans), BF16)
    edge = pltpu.VMEM((high, chans), F32)
    tap_scratch = [
        pltpu.VMEM((high + 2, wide, 3 * chans), BF16),
        pltpu.VMEM((wide + 16, chans), F32),
        pltpu.VMEM((2, high + 8, chans), F32),
    ]

    stats_one, *rims = call(
        look_kernel, (small, rows_of(2), rows_of(2), cols_of(2), cols_of(2)), 2, [edge]
    )(cells, upper)
    halo = borders(flags, *rims)
    stats_one = add_up_pair(stats_one, ("row", "col"))
    norm_one = (*stats_one, gains[0], shifts[0])

    hidden, stats_two = call(
        functools.partial(hidden_kernel, count=count),
        (shape((flat, chans), BF16), small), 10, tap_scratch, smem=1,
    )(flags, cells, *halo, weights[0], *norm_one)
    stats_two = add_up_pair(stats_two, ("row", "col"))
    norm_two = (*stats_two, gains[1], shifts[1])

    def back_conv(core, rim, weight, source, norm, which):
        return call(
            functools.partial(back_conv_kernel, count=count, which=which),
            (shape((flat, chans), F32), small), 11,
            tap_scratch + [pltpu.VMEM((3, chans, 3 * chans), BF16)], smem=1,
        )(flags, core, *rim, weight, source, *norm)

    def kernel_grad(body, core, source, norm):
        half = shape((blocks // 2, size * chans // LANES, LANES), F32)
        return call(
            functools.partial(body, count=count, size=size), (half, half), 10,
            tap_scratch + [pltpu.VMEM((chans, flat), BF16), pltpu.VMEM((padded, chans), F32)],
            smem=2,
        )(flags, places, core, *halo, source, *norm)

    give, take = give_steps(), take_steps()
    outward = len(give) - len(plan()[2])
    second = kernel_grad(second_grad_kernel, upper, hidden, norm_two)
    second, norm_two = tie(second, norm_two)

    grad_pre_two, local_two = back_conv(upper, halo, weights[1], hidden, norm_two, 1)
    second, local_two = tie(give[0](second), local_two)
    sums_two = add_up_pair(local_two, ("row", "col"))
    second, sums_two = tie(second, sums_two)

    grad_hidden, *rims = call(
        functools.partial(grad_hidden_kernel, count=count),
        (image, rows_of(1), rows_of(1), cols_of(1), cols_of(1)), 7, [edge],
    )(grad_pre_two, hidden, *norm_two[:2], *sums_two, gains[1])
    rim = borders(flags, *rims)

    first = kernel_grad(first_grad_kernel, cells, grad_hidden, norm_one)
    second = give[1](second)
    second, first, rim, grad_hidden = tie(second, first, rim, grad_hidden)

    grad_pre_one, local_one = back_conv(
        grad_hidden, rim, weights[0], cells.reshape(flat, chans), norm_one, 0
    )
    for step in give[2:outward]:
        second = step(second)
    first, second, local_one = tie(give[0](first), second, local_one)

    small_steps = [(axis, mask) for name in ("row", "col") for axis, mask in bits_of(name)]
    sums_one, other_one = local_one, None
    later = give[outward:] + take
    for level, step in enumerate(give[1:]):
        if level < len(small_steps):
            axis, mask = small_steps[level]
            other_one = swap(sums_one, axis, mask)
            if level < len(small_steps) - 1:
                sums_one = sums_one + other_one
        second = later.pop(0)(second)
        first, second, sums_one, other_one = tie(step(first), second, sums_one, other_one)
    input_grad = call(
        functools.partial(input_grad_kernel, count=count), image, 8
    )(grad_pre_one, cells, upper, *stats_one, sums_one, other_one, gains[0])

    sums = [a + b for a, b in ((sums_one, other_one), sums_two)]
    param = jnp.stack([sums[0][1], sums[0][0], sums[1][1], sums[1][0]])
    batch = bits_of("batch")
    spread = call(
        functools.partial(spread_kernel, size=size), shape((9 * chans, chans), F32), 2, smem=1
    )
    second_grad = None
    for level, step in enumerate(take):
        if level < len(batch):
            axis, mask = batch[level]
            param = param + swap(param, axis, mask)
        if later:
            second = later.pop(0)(second)
        elif second_grad is None:
            second_grad = spread(places, *second)
            first, second_grad = tie(first, second_grad)
        first = step(first)
        if level < len(take) - 1:
            if level == 0:
                first, second, input_grad = tie(first, second, input_grad)
            elif later:
                first, second = tie(first, second)
    if second_grad is None:
        second_grad = spread(places, *second)
    first_grad = spread(places, *first)
    grads = [grad.reshape(3, 3, chans, chans) for grad in (first_grad, second_grad)]
    return (input_grad[None], grads[0], grads[1], param)


def solution(mesh):
    tiled = P("batch", "row", "col", None)
    return jax.shard_map(
        per_device,
        mesh=mesh,
        in_specs=(tiled, P(), P(), P(), P(), P(), P(), tiled),
        out_specs=(tiled, P(), P(), P()),
        check_vma=False,
    )
```

time: 342 us -> 228 us (0.67)
  local copies, waits for them, and re-layouts: 64.5 us -> 17.4 us
  Pallas kernels: 110 us -> 82.7 us
  other arithmetic: 20.4 us -> 2.79 us
  waiting for transfers between devices: 73.2 us -> 60.9 us
  starting transfers between devices: 71.4 us -> 62.3 us
    pallas_call x13 -> x27, Pallas kernels: 87.1 us -> 68 us  [the longest x2 26.5 us: kernel_grad(): call(functools.partial(body, count=count, size=size), (half, half), 10, t...]
    slice x20 -> x2, local copies, waits for them, and re-layouts: 14.8 us -> 0.01 us  [per_device(): param = jnp.stack([sums[0][1], sums[0][0], sums[1][1], sums[1][0]])]
    ppermute x8 -> x0, local copies, waits for them, and re-layouts: 12.9 us -> none  [swap(): lax.ppermute(value, axis, [(i, i ^ mask) for i in range(lax.axis_size(axi...]
    add x22 -> x12, other arithmetic: 15.4 us -> 2.69 us  [the longest x6 2.05 us: add_up_pair(): value = value + swap(value, axis, other)]
    ppermute x8 -> x4, starting transfers between devices: 16.5 us -> 6.46 us  [shifted(): return lax.ppermute(value, axis, pairs)]
    concatenate x6 -> x0, local copies, waits for them, and re-layouts: 8.68 us -> none  [the longest x4 7.31 us: collect(): whole = jnp.concatenate(chunks)]
    unnamed x53 -> x49, local copies, waits for them, and re-layouts: 21.2 us -> 14.6 us
    ppermute x42 -> x44, waiting for transfers between devices: 64.6 us -> 58 us  [swap(): lax.ppermute(value, axis, [(i, i ^ mask) for i in range(lax.axis_size(axi...]
  transfers between devices with their start and end apart: 50 -> 48, of which waited for: 25 -> 28; matrix products, arithmetic and copies ran while one was open for 19% -> 3% of each run, Pallas kernels for 22% -> 19%
where the time goes in v2:
time: 228 us; the launch traced here: 227 us
  Pallas kernels  82.7 us (36%)
  starting transfers between devices  62.3 us (27%)
  waiting for transfers between devices  60.9 us (27%)
  local copies, waits for them, and re-layouts  17.4 us (8%)
  other arithmetic  2.79 us (1%)
    ppermute x44, waiting for transfers between devices, swap(): lax.ppermute(value, axis, [(i, i ^ mask) for i in range(lax.axis_size(axi...  58 us
    ppermute x44, starting transfers between devices, swap(): lax.ppermute(value, axis, [(i, i ^ mask) for i in range(lax.axis_size(axi...  55.8 us
    pallas_call x2, Pallas kernels, kernel_grad(): call(functools.partial(body, count=count, size=size), (half, half), 10, t...  26.5 us
    pallas_call x2, Pallas kernels, back_conv(): call(functools.partial(back_conv_kernel, count=count, which=which), (shap...  23.3 us
    unnamed x49, local copies, waits for them, and re-layouts  14.6 us
    pallas_call x1, Pallas kernels, per_device(): call(functools.partial(hidden_kernel, count=count), (shape((flat, chans),...  11.7 us
    pallas_call x1, Pallas kernels, per_device(): second_grad = spread(places, *second)  7.03 us
    pallas_call x1, Pallas kernels, per_device(): first_grad = spread(places, *first)  7.03 us
  transfers between devices with their start and end apart: 48, of which 28 were waited for; matrix products, arithmetic and copies ran while one was open for 3% of the time, Pallas kernels for 19%

profile of v2, /device:TPU:0, one launch (start us, length us, event | category | flops | bytes accessed | tf_op | source)
XLA Modules:
  0.0 227.2 jit_solution(16115941275845269701)
XLA Ops:
  6.8 2.4 %collective-permute-start = (bf16[2,128,320]{2,1,0:T(8,128)(2,1)}, bf16[2,128,320]{2,1,0:T(8,128)(2,1)S(1)}, u32[]{:S(2)}, u32[]{:S(2)}) collective-permute-start(bf16[2,128,320]{2,1,0:T(8,128)(2,1)} %get-tuple-element.122), channel_id=1, source_target_pairs={{0,2},{2,4},{4,6},{1,3},{3,5},{5,7},{8,10},{10,12},{12,14},{9,11},... | collective-permute-start | bytes 491528 | tf_op jit(solution)/shard_map/ppermute | solution.py:409
  10.5 3.3 %collective-permute-start.3 = (f32[8,320]{1,0:T(8,128)S(1)}, f32[8,320]{1,0:T(8,128)}, u32[]{:S(2)}, u32[]{:S(2)}) collective-permute-start(f32[8,320]{1,0:T(8,128)S(1)} %get-tuple-element.126), channel_id=1, source_target_pairs={{0,2},{2,0},{4,6},{6,4},{1,3},{3,1},{5,7},{7,5},{8,10},{10,8},{12,... | collective-permute-start | bytes 30728 | tf_op jit(solution)/shard_map/ppermute | solution.py:390
  19.2 4.0 %collective-permute-start.4 = (f32[8,320]{1,0:T(8,128)S(1)}, f32[8,320]{1,0:T(8,128)S(1)}, u32[]{:S(2)}, u32[]{:S(2)}) collective-permute-start(f32[8,320]{1,0:T(8,128)S(1)} %add.81), channel_id=1, source_target_pairs={{0,4},{2,6},{4,0},{6,2},{1,5},{3,7},{5,1},{7,3},{8,12},{10,14},{12... | collective-permute-start | bytes 30728 | tf_op jit(solution)/shard_map/ppermute | solution.py:390
  30.2 11.7 %shard_map.113 = (bf16[2048,320]{1,0:T(8,128)(2,1)S(1)}, f32[8,320]{1,0:T(8,128)S(1)}) custom-call(s32[4]{0:T(128)S(1)} %add_convert_fusion.flags, bf16[16,128,320]{2,1,0:T(8,128)(2,1)S(1)} %bitcast.13, bf16[2,128,320]{2,1,0:T(8,128)(2,1)S(1)} %collective-permute-done.above.top, bf16[2,128,320]{2,1,0:T(8,128)(2,1)S(1)} %collective-permute-done.1.below.bottom, ...), custom_call_target="tpu_custom_call" | custom-call | tf_op jit(solution)/shard_map/pallas_call | solution.py:600
  44.8 2.0 collective-permute-start.7
  46.9 2.0 collective-permute-done.7
  56.1 12.9 %shard_map.114 = (f32[32,120,128]{2,1,0:T(8,128)S(1)}, f32[32,120,128]{2,1,0:T(8,128)S(1)}) custom-call(s32[4]{0:T(128)S(1)} %copy-done.14, s32[64]{0:T(128)S(1)} %fusion.places, bf16[16,128,320]{2,1,0:T(8,128)(2,1)S(1)} %bitcast.18, bf16[2,128,320]{2,1,0:T(8,128)(2,1)S(1)} %collective-permute-done.above.top, ...), custom_call_target="tpu_custom_call" | custom-call | tf_op jit(solution)/shard_map/pallas_call | solution.py:616
  69.0 11.7 %shard_map.116 = (f32[2048,320]{1,0:T(8,128)S(1)}, f32[8,320]{1,0:T(8,128)S(1)}) custom-call(s32[4]{0:T(128)S(1)} %copy-done.14, bf16[16,128,320]{2,1,0:T(8,128)(2,1)S(1)} %bitcast.19, bf16[2,128,320]{2,1,0:T(8,128)(2,1)S(1)} %collective-permute-done.above.top, bf16[2,128,320]{2,1,0:T(8,128)(2,1)S(1)} %collective-permute-done.1.below.bottom, ...), custom_call_target="tpu_custom_call" | custom-call | tf_op jit(solution)/shard_map/pallas_call | solution.py:608
  82.3 2.0 collective-permute-start.11
  86.5 3.2 %collective-permute-done.12.sums_b = f32[8,320]{1,0:T(8,128)S(1)} collective-permute-done((f32[8,320]{1,0:T(8,128)S(1)}, f32[8,320]{1,0:T(8,128)S(1)}, u32[]{:S(2)}, u32[]{:S(2)}) %collective-permute-start.12) | collective-permute-done | bytes 10272 | tf_op jit(solution)/shard_map/ppermute | solution.py:390
  89.7 2.0 collective-permute-start.13
  96.7 1.9 collective-permute-done.16.below.bottom
  100.8 13.6 %shard_map.119 = (f32[32,120,128]{2,1,0:T(8,128)S(1)}, f32[32,120,128]{2,1,0:T(8,128)S(1)}) custom-call(s32[4]{0:T(128)S(1)} %copy-done.14, s32[64]{0:T(128)S(1)} %fusion.places, bf16[16,128,320]{2,1,0:T(8,128)(2,1)S(1)} %bitcast.14, bf16[2,128,320]{2,1,0:T(8,128)(2,1)S(1)} %collective-permute-done.above.top, ...), custom_call_target="tpu_custom_call" | custom-call | tf_op jit(solution)/shard_map/pallas_call | solution.py:616
  114.6 3.0 %collective-permute-start.18 = (f32[32,120,128]{2,1,0:T(8,128)S(1)}, f32[32,120,128]{2,1,0:T(8,128)S(1)}, u32[]{:S(2)}, u32[]{:S(2)}) collective-permute-start(f32[32,120,128]{2,1,0:T(8,128)S(1)} %get-tuple-element.166), channel_id=1, source_target_pairs={{0,2},{2,0},{4,6},{6,4},{1,3},{3,1},{5,7},{7,5},{8,10},{10,8},{12,... | collective-permute-start | bytes 5898248 | tf_op jit(solution)/shard_map/ppermute | solution.py:390
  118.7 11.7 %shard_map.123 = (f32[2048,320]{1,0:T(8,128)S(1)}, f32[8,320]{1,0:T(8,128)S(1)}) custom-call(s32[4]{0:T(128)S(1)} %copy-done.14, bf16[16,128,320]{2,1,0:T(8,128)(2,1)S(1)} %get-tuple-element.177.grad_hidden.core, bf16[1,128,320]{2,1,0:T(8,128)(2,1)S(1)} %collective-permute-done.15.above.top, bf16[1,128,320]{2,1,0:T(8,128)(2,1)S(1)} %collective-permute-done.16.below.bottom, ...), custom_call_target="tpu_custom_call" | custom-call | tf_op jit(solution)/shard_map/pallas_call | solution.py:608
  130.7 2.0 collective-permute-start.21
  136.5 4.1 %collective-permute-done.23.refs_1_ = f32[4,120,128]{2,1,0:T(8,128)S(1)} collective-permute-done((f32[4,120,128]{2,1,0:T(8,128)S(1)}, f32[4,120,128]{2,1,0:T(8,128)S(1)}, u32[]{:S(2)}, u32[]{:S(2)}) %collective-permute-start.23) | collective-permute-done | bytes 245792 | tf_op jit(solution)/shard_map/ppermute | solution.py:390
  140.6 3.1 %collective-permute-done.21.refs_1_ = f32[8,120,128]{2,1,0:T(8,128)S(1)} collective-permute-done((f32[8,120,128]{2,1,0:T(8,128)S(1)}, f32[8,120,128]{2,1,0:T(8,128)S(1)}, u32[]{:S(2)}, u32[]{:S(2)}) %collective-permute-start.21) | collective-permute-done | bytes 491552 | tf_op jit(solution)/shard_map/ppermute | solution.py:390
  146.8 2.6 %collective-permute-start.27 = (f32[2,120,128]{2,1,0:T(8,128)S(1)}, f32[2,120,128]{2,1,0:T(8,128)S(1)}, u32[]{:S(2)}, u32[]{:S(2)}) collective-permute-start(f32[2,120,128]{2,1,0:T(8,128)S(1)} %get-tuple-element.203), channel_id=1, source_target_pairs={{0,16},{8,24},{16,0},{24,8},{1,17},{9,25},{17,1},{25,9},{2,18},{10... | collective-permute-start | bytes 368648 | tf_op jit(solution)/shard_map/ppermute | solution.py:390
  150.9 2.2 collective-permute-done.28
  154.8 3.3 %collective-permute-start.30 = (bf16[2,120,128]{2,1,0:T(8,128)(2,1)S(1)}, bf16[2,120,128]{2,1,0:T(8,128)(2,1)S(1)}, u32[]{:S(2)}, u32[]{:S(2)}) collective-permute-start(bf16[2,120,128]{2,1,0:T(8,128)(2,1)S(1)} %shard_map.127.refs_0_), channel_id=1, source_target_pairs={{0,16},{8,24},{16,0},{24,8},{1,17},{9,25},{17,1},{25,9},{2,18},{10... | collective-permute-start | bytes 184328 | tf_op jit(solution)/shard_map/ppermute | solution.py:390
  161.8 2.2 collective-permute-start.33
  164.1 3.4 %collective-permute-start.32 = (f32[2,120,128]{2,1,0:T(8,128)S(1)}, f32[2,120,128]{2,1,0:T(8,128)S(1)}, u32[]{:S(2)}, u32[]{:S(2)}) collective-permute-start(f32[2,120,128]{2,1,0:T(8,128)S(1)} %get-tuple-element.212), channel_id=1, source_target_pairs={{0,16},{8,24},{16,0},{24,8},{1,17},{9,25},{17,1},{25,9},{2,18},{10... | collective-permute-start | bytes 368648 | tf_op jit(solution)/shard_map/ppermute | solution.py:390
  167.5 5.3 %collective-permute-done.32.refs_1_ = f32[2,120,128]{2,1,0:T(8,128)S(1)} collective-permute-done((f32[2,120,128]{2,1,0:T(8,128)S(1)}, f32[2,120,128]{2,1,0:T(8,128)S(1)}, u32[]{:S(2)}, u32[]{:S(2)}) %collective-permute-start.32) | collective-permute-done | bytes 122912 | tf_op jit(solution)/shard_map/ppermute | solution.py:390
  178.7 1.9 collective-permute-done.34.refs_1_
  183.3 4.3 %collective-permute-done.37.refs_1_ = bf16[4,120,128]{2,1,0:T(8,128)(2,1)S(1)} collective-permute-done((bf16[4,120,128]{2,1,0:T(8,128)(2,1)S(1)}, bf16[4,120,128]{2,1,0:T(8,128)(2,1)S(1)}, u32[]{:S(2)}, u32[]{:S(2)}) %collective-permute-start.37) | collective-permute-done | bytes 122912 | tf_op jit(solution)/shard_map/ppermute | solution.py:390
  190.1 3.4 %collective-permute-done.40.refs_1_ = bf16[4,120,128]{2,1,0:T(8,128)(2,1)S(1)} collective-permute-done((bf16[4,120,128]{2,1,0:T(8,128)(2,1)S(1)}, bf16[4,120,128]{2,1,0:T(8,128)(2,1)S(1)}, u32[]{:S(2)}, u32[]{:S(2)}) %collective-permute-start.40) | collective-permute-done | bytes 122912 | tf_op jit(solution)/shard_map/ppermute | solution.py:390
  194.5 7.0 %shard_map.138 = f32[2880,320]{1,0:T(8,128)} custom-call(s32[64]{0:T(128)S(1)} %fusion.places, bf16[32,120,128]{2,1,0:T(8,128)(2,1)S(1)} %shard_map.136.mine, bf16[32,120,128]{2,1,0:T(8,128)(2,1)S(1)} %collective-permute-done.42.other), custom_call_target="tpu_custom_call" | custom-call | tf_op jit(solution)/shard_map/pallas_call | solution.py:678
  203.6 5.1 %collective-permute-done.43.refs_1_ = bf16[8,120,128]{2,1,0:T(8,128)(2,1)S(1)} collective-permute-done((bf16[8,120,128]{2,1,0:T(8,128)(2,1)S(1)}, bf16[8,120,128]{2,1,0:T(8,128)(2,1)S(1)}, u32[]{:S(2)}, u32[]{:S(2)}) %collective-permute-start.43) | collective-permute-done | bytes 245792 | tf_op jit(solution)/shard_map/ppermute | solution.py:390
  210.4 2.9 %collective-permute-done.46 = f32[4,320]{1,0:T(4,128)S(1)} collective-permute-done((f32[4,320]{1,0:T(4,128)S(1)}, f32[4,320]{1,0:T(4,128)S(1)}, u32[]{:S(2)}, u32[]{:S(2)}) %collective-permute-start.46) | collective-permute-done | bytes 5152 | tf_op jit(solution)/shard_map/ppermute | solution.py:390
  214.2 3.7 %collective-permute-done.47 = f32[4,320]{1,0:T(4,128)S(1)} collective-permute-done((f32[4,320]{1,0:T(4,128)S(1)}, f32[4,320]{1,0:T(4,128)S(1)}, u32[]{:S(2)}, u32[]{:S(2)}) %collective-permute-start.47) | collective-permute-done | bytes 5152 | tf_op jit(solution)/shard_map/ppermute | solution.py:390
  220.2 7.0 %shard_map.140 = f32[2880,320]{1,0:T(8,128)} custom-call(s32[64]{0:T(128)S(1)} %copy-done.22, bf16[32,120,128]{2,1,0:T(8,128)(2,1)S(1)} %shard_map.139.mine, bf16[32,120,128]{2,1,0:T(8,128)(2,1)S(1)} %collective-permute-done.45.other), custom_call_target="tpu_custom_call" | custom-call | tf_op jit(solution)/shard_map/pallas_call | solution.py:688
  (164 shorter events, 75.2 us)
Async XLA Ops:
  6.8 7.1 %collective-permute-start = (bf16[2,128,320]{2,1,0:T(8,128)(2,1)}, bf16[2,128,320]{2,1,0:T(8,128)(2,1)S(1)}, u32[]{:S(2)}, u32[]{:S(2)}) collective-permute-start(bf16[2,128,320]{2,1,0:T(8,128)(2,1)} %get-tuple-element.122), channel_id=1, source_target_pairs={{0,2},{2,4},{4,6},{1,3},{3,5},{5,7},{8,10},{10,12},{12,14},{9,11},... | collective-permute-start | bytes 491528 | tf_op jit(solution)/shard_map/ppermute | solution.py:409
  9.2 5.6 %collective-permute-start.1 = (bf16[2,128,320]{2,1,0:T(8,128)(2,1)}, bf16[2,128,320]{2,1,0:T(8,128)(2,1)S(1)}, u32[]{:S(2)}, u32[]{:S(2)}) collective-permute-start(bf16[2,128,320]{2,1,0:T(8,128)(2,1)} %get-tuple-element.123), channel_id=1, source_target_pairs={{2,0},{4,2},{6,4},{3,1},{5,3},{7,5},{10,8},{12,10},{14,12},{11,9},... | collective-permute-start | bytes 491528 | tf_op jit(solution)/shard_map/ppermute | solution.py:409
  10.5 8.0 %collective-permute-start.3 = (f32[8,320]{1,0:T(8,128)S(1)}, f32[8,320]{1,0:T(8,128)}, u32[]{:S(2)}, u32[]{:S(2)}) collective-permute-start(f32[8,320]{1,0:T(8,128)S(1)} %get-tuple-element.126), channel_id=1, source_target_pairs={{0,2},{2,0},{4,6},{6,4},{1,3},{3,1},{5,7},{7,5},{8,10},{10,8},{12,... | collective-permute-start | bytes 30728 | tf_op jit(solution)/shard_map/ppermute | solution.py:390
  16.9 11.7 %collective-permute-start.2 = (bf16[2,24,320]{2,1,0:T(8,128)(2,1)S(1)}, bf16[2,24,320]{2,1,0:T(8,128)(2,1)S(1)}, u32[]{:S(2)}, u32[]{:S(2)}) collective-permute-start(bf16[2,24,320]{2,1,0:T(8,128)(2,1)S(1)} %shard_map.112), channel_id=1, source_target_pairs={{0,1},{1,0},{2,3},{3,2},{4,5},{5,4},{6,7},{7,6},{8,9},{9,8},{10,11... | collective-permute-start | bytes 92168 | tf_op jit(solution)/shard_map/ppermute | solution.py:390
  19.2 5.7 %collective-permute-start.4 = (f32[8,320]{1,0:T(8,128)S(1)}, f32[8,320]{1,0:T(8,128)S(1)}, u32[]{:S(2)}, u32[]{:S(2)}) collective-permute-start(f32[8,320]{1,0:T(8,128)S(1)} %add.81), channel_id=1, source_target_pairs={{0,4},{2,6},{4,0},{6,2},{1,5},{3,7},{5,1},{7,3},{8,12},{10,14},{12... | collective-permute-start | bytes 30728 | tf_op jit(solution)/shard_map/ppermute | solution.py:390
  68.9 11.7 %collective-permute-start.9 = (f32[32,120,128]{2,1,0:T(8,128)S(1)}, f32[32,120,128]{2,1,0:T(8,128)S(1)}, u32[]{:S(2)}, u32[]{:S(2)}) collective-permute-start(f32[32,120,128]{2,1,0:T(8,128)S(1)} %get-tuple-element.132), channel_id=1, source_target_pairs={{0,2},{2,0},{4,6},{6,4},{1,3},{3,1},{5,7},{7,5},{8,10},{10,8},{12,... | collective-permute-start | bytes 5898248 | tf_op jit(solution)/shard_map/ppermute | solution.py:390
  89.7 24.8 %collective-permute-start.13 = (f32[8,120,128]{2,1,0:T(8,128)S(1)}, f32[8,120,128]{2,1,0:T(8,128)S(1)}, u32[]{:S(2)}, u32[]{:S(2)}) collective-permute-start(f32[8,120,128]{2,1,0:T(8,128)S(1)} %get-tuple-element.148), channel_id=1, source_target_pairs={{0,4},{2,6},{4,0},{6,2},{1,5},{3,7},{5,1},{7,3},{8,12},{10,14},{12... | collective-permute-start | bytes 1474568 | tf_op jit(solution)/shard_map/ppermute | solution.py:390
  91.7 22.8 %collective-permute-start.14 = (f32[8,120,128]{2,1,0:T(8,128)S(1)}, f32[8,120,128]{2,1,0:T(8,128)S(1)}, u32[]{:S(2)}, u32[]{:S(2)}) collective-permute-start(f32[8,120,128]{2,1,0:T(8,128)S(1)} %get-tuple-element.150), channel_id=1, source_target_pairs={{0,1},{1,0},{2,3},{3,2},{4,5},{5,4},{6,7},{7,6},{8,9},{9,8},{10,11... | collective-permute-start | bytes 1474568 | tf_op jit(solution)/shard_map/ppermute | solution.py:390
  99.2 15.4 %collective-permute-start.17 = (bf16[1,24,320]{2,1,0:T(8,128)(2,1)S(1)}, bf16[1,24,320]{2,1,0:T(8,128)(2,1)S(1)}, u32[]{:S(2)}, u32[]{:S(2)}) collective-permute-start(bf16[1,24,320]{2,1,0:T(8,128)(2,1)S(1)} %shard_map.120), channel_id=1, source_target_pairs={{0,1},{1,0},{2,3},{3,2},{4,5},{5,4},{6,7},{7,6},{8,9},{9,8},{10,11... | collective-permute-start | bytes 46088 | tf_op jit(solution)/shard_map/ppermute | solution.py:390
  114.6 15.8 %collective-permute-start.18 = (f32[32,120,128]{2,1,0:T(8,128)S(1)}, f32[32,120,128]{2,1,0:T(8,128)S(1)}, u32[]{:S(2)}, u32[]{:S(2)}) collective-permute-start(f32[32,120,128]{2,1,0:T(8,128)S(1)} %get-tuple-element.166), channel_id=1, source_target_pairs={{0,2},{2,0},{4,6},{6,4},{1,3},{3,1},{5,7},{7,5},{8,10},{10,8},{12,... | collective-permute-start | bytes 5898248 | tf_op jit(solution)/shard_map/ppermute | solution.py:390
  117.6 12.7 %collective-permute-start.19 = (f32[4,120,128]{2,1,0:T(8,128)S(1)}, f32[4,120,128]{2,1,0:T(8,128)S(1)}, u32[]{:S(2)}, u32[]{:S(2)}) collective-permute-start(f32[4,120,128]{2,1,0:T(8,128)S(1)} %get-tuple-element.172), channel_id=1, source_target_pairs={{0,1},{1,0},{2,3},{3,2},{4,5},{5,4},{6,7},{7,6},{8,9},{9,8},{10,11... | collective-permute-start | bytes 737288 | tf_op jit(solution)/shard_map/ppermute | solution.py:390
  118.6 11.8 %collective-permute-start.20 = (f32[4,120,128]{2,1,0:T(8,128)S(1)}, f32[4,120,128]{2,1,0:T(8,128)S(1)}, u32[]{:S(2)}, u32[]{:S(2)}) collective-permute-start(f32[4,120,128]{2,1,0:T(8,128)S(1)} %get-tuple-element.174), channel_id=1, source_target_pairs={{0,4},{2,6},{4,0},{6,2},{1,5},{3,7},{5,1},{7,3},{8,12},{10,14},{12... | collective-permute-start | bytes 737288 | tf_op jit(solution)/shard_map/ppermute | solution.py:390
  130.7 13.1 %collective-permute-start.21 = (f32[8,120,128]{2,1,0:T(8,128)S(1)}, f32[8,120,128]{2,1,0:T(8,128)S(1)}, u32[]{:S(2)}, u32[]{:S(2)}) collective-permute-start(f32[8,120,128]{2,1,0:T(8,128)S(1)} %get-tuple-element.184), channel_id=1, source_target_pairs={{0,4},{2,6},{4,0},{6,2},{1,5},{3,7},{5,1},{7,3},{8,12},{10,14},{12... | collective-permute-start | bytes 1474568 | tf_op jit(solution)/shard_map/ppermute | solution.py:390
  132.6 12.4 %collective-permute-start.22 = (f32[8,120,128]{2,1,0:T(8,128)S(1)}, f32[8,120,128]{2,1,0:T(8,128)S(1)}, u32[]{:S(2)}, u32[]{:S(2)}) collective-permute-start(f32[8,120,128]{2,1,0:T(8,128)S(1)} %get-tuple-element.186), channel_id=1, source_target_pairs={{0,1},{1,0},{2,3},{3,2},{4,5},{5,4},{6,7},{7,6},{8,9},{9,8},{10,11... | collective-permute-start | bytes 1474568 | tf_op jit(solution)/shard_map/ppermute | solution.py:390
  133.7 6.8 %collective-permute-start.23 = (f32[4,120,128]{2,1,0:T(8,128)S(1)}, f32[4,120,128]{2,1,0:T(8,128)S(1)}, u32[]{:S(2)}, u32[]{:S(2)}) collective-permute-start(f32[4,120,128]{2,1,0:T(8,128)S(1)} %get-tuple-element.192), channel_id=1, source_target_pairs={{0,8},{8,0},{16,24},{24,16},{1,9},{9,1},{17,25},{25,17},{2,10},{10... | collective-permute-start | bytes 737288 | tf_op jit(solution)/shard_map/ppermute | solution.py:390
  145.1 8.9 %collective-permute-start.25 = (f32[4,120,128]{2,1,0:T(8,128)S(1)}, f32[4,120,128]{2,1,0:T(8,128)S(1)}, u32[]{:S(2)}, u32[]{:S(2)}) collective-permute-start(f32[4,120,128]{2,1,0:T(8,128)S(1)} %get-tuple-element.197), channel_id=1, source_target_pairs={{0,1},{1,0},{2,3},{3,2},{4,5},{5,4},{6,7},{7,6},{8,9},{9,8},{10,11... | collective-permute-start | bytes 737288 | tf_op jit(solution)/shard_map/ppermute | solution.py:390
  146.3 7.7 %collective-permute-start.26 = (f32[4,120,128]{2,1,0:T(8,128)S(1)}, f32[4,120,128]{2,1,0:T(8,128)S(1)}, u32[]{:S(2)}, u32[]{:S(2)}) collective-permute-start(f32[4,120,128]{2,1,0:T(8,128)S(1)} %get-tuple-element.199), channel_id=1, source_target_pairs={{0,4},{2,6},{4,0},{6,2},{1,5},{3,7},{5,1},{7,3},{8,12},{10,14},{12... | collective-permute-start | bytes 737288 | tf_op jit(solution)/shard_map/ppermute | solution.py:390
  146.8 7.2 %collective-permute-start.27 = (f32[2,120,128]{2,1,0:T(8,128)S(1)}, f32[2,120,128]{2,1,0:T(8,128)S(1)}, u32[]{:S(2)}, u32[]{:S(2)}) collective-permute-start(f32[2,120,128]{2,1,0:T(8,128)S(1)} %get-tuple-element.203), channel_id=1, source_target_pairs={{0,16},{8,24},{16,0},{24,8},{1,17},{9,25},{17,1},{25,9},{2,18},{10... | collective-permute-start | bytes 368648 | tf_op jit(solution)/shard_map/ppermute | solution.py:390
  154.1 7.5 %collective-permute-start.29 = (f32[4,120,128]{2,1,0:T(8,128)S(1)}, f32[4,120,128]{2,1,0:T(8,128)S(1)}, u32[]{:S(2)}, u32[]{:S(2)}) collective-permute-start(f32[4,120,128]{2,1,0:T(8,128)S(1)} %get-tuple-element.206), channel_id=1, source_target_pairs={{0,8},{8,0},{16,24},{24,16},{1,9},{9,1},{17,25},{25,17},{2,10},{10... | collective-permute-start | bytes 737288 | tf_op jit(solution)/shard_map/ppermute | solution.py:390
  154.8 5.6 %collective-permute-start.30 = (bf16[2,120,128]{2,1,0:T(8,128)(2,1)S(1)}, bf16[2,120,128]{2,1,0:T(8,128)(2,1)S(1)}, u32[]{:S(2)}, u32[]{:S(2)}) collective-permute-start(bf16[2,120,128]{2,1,0:T(8,128)(2,1)S(1)} %shard_map.127.refs_0_), channel_id=1, source_target_pairs={{0,16},{8,24},{16,0},{24,8},{1,17},{9,25},{17,1},{25,9},{2,18},{10... | collective-permute-start | bytes 184328 | tf_op jit(solution)/shard_map/ppermute | solution.py:390
  161.8 5.6 %collective-permute-start.33 = (bf16[4,120,128]{2,1,0:T(8,128)(2,1)S(1)}, bf16[4,120,128]{2,1,0:T(8,128)(2,1)S(1)}, u32[]{:S(2)}, u32[]{:S(2)}) collective-permute-start(bf16[4,120,128]{2,1,0:T(8,128)(2,1)S(1)} %shard_map.129.refs_0_), channel_id=1, source_target_pairs={{0,8},{8,0},{16,24},{24,16},{1,9},{9,1},{17,25},{25,17},{2,10},{10... | collective-permute-start | bytes 368648 | tf_op jit(solution)/shard_map/ppermute | solution.py:390
  164.1 8.7 %collective-permute-start.32 = (f32[2,120,128]{2,1,0:T(8,128)S(1)}, f32[2,120,128]{2,1,0:T(8,128)S(1)}, u32[]{:S(2)}, u32[]{:S(2)}) collective-permute-start(f32[2,120,128]{2,1,0:T(8,128)S(1)} %get-tuple-element.212), channel_id=1, source_target_pairs={{0,16},{8,24},{16,0},{24,8},{1,17},{9,25},{17,1},{25,9},{2,18},{10... | collective-permute-start | bytes 368648 | tf_op jit(solution)/shard_map/ppermute | solution.py:390
  172.8 7.8 %collective-permute-start.35 = (bf16[4,120,128]{2,1,0:T(8,128)(2,1)S(1)}, bf16[4,120,128]{2,1,0:T(8,128)(2,1)S(1)}, u32[]{:S(2)}, u32[]{:S(2)}) collective-permute-start(bf16[4,120,128]{2,1,0:T(8,128)(2,1)S(1)} %get-tuple-element.219.refs_0_), channel_id=1, source_target_pairs={{0,1},{1,0},{2,3},{3,2},{4,5},{5,4},{6,7},{7,6},{8,9},{9,8},{10,11... | collective-permute-start | bytes 368648 | tf_op jit(solution)/shard_map/ppermute | solution.py:390
  173.7 6.9 %collective-permute-start.36 = (bf16[4,120,128]{2,1,0:T(8,128)(2,1)S(1)}, bf16[4,120,128]{2,1,0:T(8,128)(2,1)S(1)}, u32[]{:S(2)}, u32[]{:S(2)}) collective-permute-start(bf16[4,120,128]{2,1,0:T(8,128)(2,1)S(1)} %get-tuple-element.220.refs_2_), channel_id=1, source_target_pairs={{0,4},{2,6},{4,0},{6,2},{1,5},{3,7},{5,1},{7,3},{8,12},{10,14},{12... | collective-permute-start | bytes 368648 | tf_op jit(solution)/shard_map/ppermute | solution.py:390
  175.1 5.5 %collective-permute-start.34 = (bf16[2,120,128]{2,1,0:T(8,128)(2,1)S(1)}, bf16[2,120,128]{2,1,0:T(8,128)(2,1)S(1)}, u32[]{:S(2)}, u32[]{:S(2)}) collective-permute-start(bf16[2,120,128]{2,1,0:T(8,128)(2,1)S(1)} %shard_map.130.refs_0_), channel_id=1, source_target_pairs={{0,16},{8,24},{16,0},{24,8},{1,17},{9,25},{17,1},{25,9},{2,18},{10... | collective-permute-start | bytes 184328 | tf_op jit(solution)/shard_map/ppermute | solution.py:390
  180.6 6.9 %collective-permute-start.38 = (bf16[8,120,128]{2,1,0:T(8,128)(2,1)S(1)}, bf16[8,120,128]{2,1,0:T(8,128)(2,1)S(1)}, u32[]{:S(2)}, u32[]{:S(2)}) collective-permute-start(bf16[8,120,128]{2,1,0:T(8,128)(2,1)S(1)} %get-tuple-element.230.refs_0_), channel_id=1, source_target_pairs={{0,4},{2,6},{4,0},{6,2},{1,5},{3,7},{5,1},{7,3},{8,12},{10,14},{12... | collective-permute-start | bytes 737288 | tf_op jit(solution)/shard_map/ppermute | solution.py:390
  181.4 6.2 %collective-permute-start.39 = (bf16[8,120,128]{2,1,0:T(8,128)(2,1)S(1)}, bf16[8,120,128]{2,1,0:T(8,128)(2,1)S(1)}, u32[]{:S(2)}, u32[]{:S(2)}) collective-permute-start(bf16[8,120,128]{2,1,0:T(8,128)(2,1)S(1)} %get-tuple-element.231.refs_2_), channel_id=1, source_target_pairs={{0,1},{1,0},{2,3},{3,2},{4,5},{5,4},{6,7},{7,6},{8,9},{9,8},{10,11... | collective-permute-start | bytes 737288 | tf_op jit(solution)/shard_map/ppermute | solution.py:390
  187.7 6.8 %collective-permute-start.42 = (bf16[32,120,128]{2,1,0:T(8,128)(2,1)S(1)}, bf16[32,120,128]{2,1,0:T(8,128)(2,1)S(1)}, u32[]{:S(2)}, u32[]{:S(2)}) collective-permute-start(bf16[32,120,128]{2,1,0:T(8,128)(2,1)S(1)} %shard_map.136.mine), channel_id=1, source_target_pairs={{0,2},{2,0},{4,6},{6,4},{1,3},{3,1},{5,7},{7,5},{8,10},{10,8},{12,... | collective-permute-start | bytes 2949128 | tf_op jit(solution)/shard_map/ppermute | solution.py:390
  187.8 5.7 %collective-permute-start.40 = (bf16[4,120,128]{2,1,0:T(8,128)(2,1)S(1)}, bf16[4,120,128]{2,1,0:T(8,128)(2,1)S(1)}, u32[]{:S(2)}, u32[]{:S(2)}) collective-permute-start(bf16[4,120,128]{2,1,0:T(8,128)(2,1)S(1)} %get-tuple-element.232.refs_0_), channel_id=1, source_target_pairs={{0,1},{1,0},{2,3},{3,2},{4,5},{5,4},{6,7},{7,6},{8,9},{9,8},{10,11... | collective-permute-start | bytes 368648 | tf_op jit(solution)/shard_map/ppermute | solution.py:390
  201.6 7.2 %collective-permute-start.43 = (bf16[8,120,128]{2,1,0:T(8,128)(2,1)S(1)}, bf16[8,120,128]{2,1,0:T(8,128)(2,1)S(1)}, u32[]{:S(2)}, u32[]{:S(2)}) collective-permute-start(bf16[8,120,128]{2,1,0:T(8,128)(2,1)S(1)} %get-tuple-element.237.refs_0_), channel_id=1, source_target_pairs={{0,4},{2,6},{4,0},{6,2},{1,5},{3,7},{5,1},{7,3},{8,12},{10,14},{12... | collective-permute-start | bytes 737288 | tf_op jit(solution)/shard_map/ppermute | solution.py:390
  202.6 6.9 %collective-permute-start.44 = (bf16[8,120,128]{2,1,0:T(8,128)(2,1)S(1)}, bf16[8,120,128]{2,1,0:T(8,128)(2,1)S(1)}, u32[]{:S(2)}, u32[]{:S(2)}) collective-permute-start(bf16[8,120,128]{2,1,0:T(8,128)(2,1)S(1)} %get-tuple-element.238.refs_2_), channel_id=1, source_target_pairs={{0,1},{1,0},{2,3},{3,2},{4,5},{5,4},{6,7},{7,6},{8,9},{9,8},{10,11... | collective-permute-start | bytes 737288 | tf_op jit(solution)/shard_map/ppermute | solution.py:390
  209.5 10.6 %collective-permute-start.45 = (bf16[32,120,128]{2,1,0:T(8,128)(2,1)S(1)}, bf16[32,120,128]{2,1,0:T(8,128)(2,1)S(1)}, u32[]{:S(2)}, u32[]{:S(2)}) collective-permute-start(bf16[32,120,128]{2,1,0:T(8,128)(2,1)S(1)} %shard_map.139.mine), channel_id=1, source_target_pairs={{0,2},{2,0},{4,6},{6,4},{1,3},{3,1},{5,7},{7,5},{8,10},{10,8},{12,... | collective-permute-start | bytes 2949128 | tf_op jit(solution)/shard_map/ppermute | solution.py:390
  (39 other events, 374.3 us)
